TPU v7x, 256 devices: a whole 4x4x8 slice. The times are simulated.
256 devices in a mesh: section: 2 (over y_hi), seq: 16 (over z, y_lo), tp: 8 (over x, core).
Axes of the slice: x: 4, y: 4 (y_hi: 2, y_lo: 2; y = y_hi * 2 + y_lo), z: 8, core: 2. Of those that a mesh axis runs over, the one named last changes fastest.
Arguments:
- layer_input: bfloat16 [2, 4096, 4096], P('section', 'seq'), may hold values from -500 to 500
- upstream: bfloat16 [2, 4096, 4096], P('section', 'seq'), may hold values from -6 to 6
- norm_gain: bfloat16 [2, 4096], P('section'), may hold values from 0.5 to 1.5
- query_weight: bfloat16 [2, 4096, 2048], P('section', 'seq', 'tp'), may hold values from -0.0625 to 0.0625
- key_weight: bfloat16 [2, 4096, 1024], P('section', 'seq', 'tp'), may hold values from -0.0625 to 0.0625
- value_weight: bfloat16 [2, 4096, 1024], P('section', 'seq', 'tp'), may hold values from -0.09375 to 0.09375
- output_weight: bfloat16 [2, 4096, 2048], P('section', 'seq', 'tp'), may hold values from -0.125 to 0.125
Outputs:
- passed_grad: bfloat16 [2, 4096, 4096], P('section', 'seq')
- query_grad: bfloat16 [2, 4096, 2048], P('section', 'seq', 'tp')
- key_grad: bfloat16 [2, 4096, 1024], P('section', 'seq', 'tp')
- value_grad: bfloat16 [2, 4096, 1024], P('section', 'seq', 'tp')
- output_grad: bfloat16 [2, 4096, 2048], P('section', 'seq', 'tp')
- gain_grad: float32 [2, 4096], P('section', 'tp')
All inputs are finite; a program needn't handle non-finite values.
Results may differ from a plain program's by a relative error of at most 0.023.
Values may be sent and summed in bfloat16 or wider, within the bound.
A program may use at most 64 MiB of HBM per device.

v0:
```python
import math

import jax
import jax.numpy as jnp
from jax import lax
from jax.sharding import Mesh
from jax.sharding import PartitionSpec as P

HEAD_DIM = 128
WINDOW = 2048
SEQ = ("seq_0", "seq_1")


epsilon = 1e-05


def in_one_piece(arrays, axis, dim, along):
    both = jnp.concatenate(arrays, axis=along)
    out, at, done = (lax.all_gather(both, axis, axis=dim, tiled=True), 0, [])
    for a in arrays:
        done.append(lax.slice_in_dim(out, at, at + a.shape[along], axis=along))
        at += a.shape[along]
    return tuple(done)


def shifted(value, axis, steps):
    count = lax.axis_size(axis)
    leading, last = (max(0, -steps), min(count, count - steps))
    return lax.ppermute(value, axis, [(source, source + steps) for source in range(leading, last)])


def cut_along(shard, dim, count):
    before, after = (shard.shape[:dim], shard.shape[dim + 1 :])
    return jnp.moveaxis(shard.reshape(*before, count, -1, *after), dim, 0)


def summed_on_arrival(shard, axis, dim):
    count = lax.axis_size(axis)
    parts = lax.all_to_all(cut_along(shard, dim, count), axis, 0, 0, tiled=True)
    return jnp.sum(parts.astype(jnp.float32), axis=0)


def sent_to_all(shard, axis):
    copies = jnp.broadcast_to(shard, (lax.axis_size(axis), *shard.shape))
    return lax.all_to_all(copies, axis, split_axis=0, concat_axis=0, tiled=True)


def of_everyone(shard, axis):
    return sent_to_all(shard, axis).sum(axis=0)


def joined_along(parts, dim):
    parts = jnp.moveaxis(parts, 0, dim)
    lengths = parts.shape
    return parts.reshape(*lengths[:dim], lengths[dim] * lengths[dim + 1], *lengths[dim + 2 :])


def collect(shard, axis, dim):
    return joined_along(sent_to_all(shard, axis), dim)


def shifted_2(value, axis, steps):
    count = lax.axis_size(axis)
    pairs = [(source, (source + steps) % count) for source in range(count)]
    return lax.ppermute(value, axis, pairs)


def sum_by_axis(terms, axes):
    so_far = terms.astype(jnp.bfloat16)
    for axis in axes:
        so_far = lax.psum_scatter(so_far, axis, scatter_dimension=0, tiled=True)
    return so_far.astype(jnp.float32)


def rotate(values, positions, direction_sign):
    half_width = values.shape[-1] // 2
    frequency = jnp.exp(
        jnp.arange(half_width, dtype=jnp.float32) * (-2.0 * math.log(10000.0) / values.shape[-1])
    )
    angles = positions[:, None] * frequency[None, :]
    cosine = jnp.cos(angles)[:, None, :]
    sine_table = direction_sign * jnp.sin(angles)[:, None, :]
    first_half = values[..., :half_width]
    second_half = values[..., half_width:]
    return jnp.concatenate(
        [
            first_half * cosine - second_half * sine_table,
            second_half * cosine + first_half * sine_table,
        ],
        axis=-1,
    )


def contract_rows(left_side, right_side):
    return lax.dot_general(
        left_side, right_side, (((0,), (0,)), ((), ())), preferred_element_type=jnp.float32
    )


def contract_last(left_side, right_side):
    return lax.dot_general(
        left_side, right_side, (((1,), (1,)), ((), ())), preferred_element_type=jnp.float32
    )


def per_device(
    layer_input, upstream, norm_gain, query_weight, key_weight, value_weight, output_weight
):
    input_rows = layer_input[0]
    upstream_rows = upstream[0]
    block_rows = input_rows.shape[0]
    model_width = input_rows.shape[1]
    seq_count = lax.axis_size(SEQ)
    seq_index = lax.axis_index(SEQ)
    tp_count = lax.axis_size("tp")
    tp_index = lax.axis_index("tp")
    query_cols = query_weight.shape[2]
    kv_cols = key_weight.shape[2]
    local_heads = query_cols // HEAD_DIM
    local_groups = kv_cols // HEAD_DIM
    group_size = local_heads // local_groups
    halo_blocks = min((WINDOW + block_rows - 2) // block_rows, seq_count - 1)
    span_rows = (halo_blocks + 1) * block_rows
    score_scale = 1.0 / math.sqrt(HEAD_DIM)
    share_width = model_width // tp_count
    input_values = input_rows.astype(jnp.float32)
    inverse_norm = lax.rsqrt(
        jnp.mean(input_values * input_values, axis=-1, keepdims=True) + epsilon
    )
    gain_values = norm_gain[0].astype(jnp.float32)
    normed = (input_values * inverse_norm * gain_values).astype(jnp.bfloat16)
    gathered = in_one_piece((query_weight, key_weight, value_weight, output_weight), SEQ, 1, 2)
    query_full = gathered[0][0]
    key_full = gathered[1][0]
    value_full = gathered[2][0]
    output_full = gathered[3][0]
    first_position = seq_index * block_rows
    positions = (first_position + jnp.arange(block_rows)).astype(jnp.float32)
    query_vectors = rotate(
        jnp.dot(normed, query_full, preferred_element_type=jnp.float32).reshape(
            block_rows, local_heads, HEAD_DIM
        ),
        positions,
        1.0,
    ).astype(jnp.bfloat16)
    key_vectors = rotate(
        jnp.dot(normed, key_full, preferred_element_type=jnp.float32).reshape(
            block_rows, local_groups, HEAD_DIM
        ),
        positions,
        1.0,
    ).astype(jnp.bfloat16)
    value_vectors = (
        jnp.dot(normed, value_full, preferred_element_type=jnp.float32)
        .astype(jnp.bfloat16)
        .reshape(block_rows, local_groups, HEAD_DIM)
    )
    attn_delta = (
        jnp.dot(upstream_rows, output_full, preferred_element_type=jnp.float32)
        .astype(jnp.bfloat16)
        .reshape(block_rows, local_heads, HEAD_DIM)
    )
    everything = in_one_piece((key_vectors, value_vectors), SEQ, 0, 1)
    padding = jnp.zeros((halo_blocks * block_rows, local_groups, HEAD_DIM), jnp.bfloat16)
    key_slab = lax.dynamic_slice_in_dim(
        jnp.concatenate([padding, everything[0]], axis=0), first_position, span_rows, 0
    )
    value_slab = lax.dynamic_slice_in_dim(
        jnp.concatenate([padding, everything[1]], axis=0), first_position, span_rows, 0
    )
    query_position = first_position + jnp.arange(block_rows)
    key_position = (seq_index - halo_blocks) * block_rows + jnp.arange(span_rows)
    allowed = (
        (key_position[None, :] <= query_position[:, None])
        & (key_position[None, :] > query_position[:, None] - WINDOW)
        & (key_position[None, :] >= 0)
    )
    attended_parts = []
    query_grad_parts = []
    key_accum = [jnp.zeros((span_rows, HEAD_DIM), jnp.float32)]
    value_accum = [jnp.zeros((span_rows, HEAD_DIM), jnp.float32)]
    for head_index in range(local_heads):
        group_index = head_index // group_size
        query_head = query_vectors[:, head_index, :]
        keys_head = key_slab[:, group_index, :]
        values_head = value_slab[:, group_index, :]
        delta_head = attn_delta[:, head_index, :]
        scores = jnp.where(allowed, contract_last(query_head, keys_head) * score_scale, -1e30)
        row_peak = jnp.max(scores, axis=-1, keepdims=True)
        exponent_terms = jnp.exp(scores - row_peak)
        softmax_probs = exponent_terms / jnp.sum(exponent_terms, axis=-1, keepdims=True)
        rounded_probs = softmax_probs.astype(jnp.bfloat16)
        attended_head = jnp.dot(
            rounded_probs, values_head, preferred_element_type=jnp.float32
        ).astype(jnp.bfloat16)
        softmax_delta = contract_last(delta_head, values_head)
        row_delta = jnp.sum(
            delta_head.astype(jnp.float32) * attended_head.astype(jnp.float32),
            axis=-1,
            keepdims=True,
        )
        score_delta = (softmax_probs * (softmax_delta - row_delta) * score_scale).astype(
            jnp.bfloat16
        )
        query_grad_parts.append(jnp.dot(score_delta, keys_head, preferred_element_type=jnp.float32))
        key_accum[group_index] = key_accum[group_index] + contract_rows(score_delta, query_head)
        value_accum[group_index] = value_accum[group_index] + contract_rows(
            rounded_probs, delta_head
        )
        attended_parts.append(attended_head)
    key_slab_grad = jnp.stack(key_accum, axis=1)
    value_slab_grad = jnp.stack(value_accum, axis=1)
    key_total = key_slab_grad[halo_blocks * block_rows :]
    value_total = value_slab_grad[halo_blocks * block_rows :]
    for distance in range(1, halo_blocks + 1):
        first_row = (halo_blocks - distance) * block_rows
        arrived = (
            shifted(
                key_slab_grad[first_row : first_row + block_rows].astype(jnp.bfloat16),
                SEQ,
                -distance,
            ).astype(jnp.float32),
            shifted(
                value_slab_grad[first_row : first_row + block_rows].astype(jnp.bfloat16),
                SEQ,
                -distance,
            ).astype(jnp.float32),
        )
        key_total = key_total + arrived[0]
        value_total = value_total + arrived[1]
    query_delta = (
        rotate(jnp.stack(query_grad_parts, axis=1), positions, -1.0)
        .astype(jnp.bfloat16)
        .reshape(block_rows, query_cols)
    )
    key_delta = rotate(key_total, positions, -1.0).astype(jnp.bfloat16).reshape(block_rows, kv_cols)
    value_delta = value_total.astype(jnp.bfloat16).reshape(block_rows, kv_cols)
    attended_flat = jnp.stack(attended_parts, axis=1).reshape(block_rows, query_cols)
    normed_partial = (
        contract_last(query_delta, query_full)
        + contract_last(key_delta, key_full)
        + contract_last(value_delta, value_full)
    )
    share_start = tp_index * share_width
    input_share = lax.dynamic_slice_in_dim(input_values, share_start, share_width, 1)
    cube_norm = inverse_norm * inverse_norm * inverse_norm
    delta_share = summed_on_arrival(normed_partial.astype(jnp.bfloat16), "tp", 1)
    gain_share = lax.dynamic_slice_in_dim(gain_values, share_start, share_width, 0)
    row_dot = of_everyone(
        jnp.sum(gain_share * delta_share * input_share, axis=-1, keepdims=True), "tp"
    )
    upstream_share = lax.dynamic_slice_in_dim(upstream_rows, share_start, share_width, 1).astype(
        jnp.float32
    )
    delta_piece = (
        upstream_share
        + inverse_norm * gain_share * delta_share
        - input_share * cube_norm * row_dot / model_width
    ).astype(jnp.bfloat16)
    input_delta = collect(delta_piece, "tp", 1)
    gain_part = jnp.sum(delta_share * input_share * inverse_norm, axis=0)
    gain_total = of_everyone(gain_part, SEQ)
    passed = shifted_2(input_delta[None], "section", -1)
    deltas_all = jnp.concatenate([query_delta, key_delta, value_delta], axis=1)
    summed_grads = sum_by_axis(
        jnp.concatenate(
            [contract_rows(normed, deltas_all), contract_rows(upstream_rows, attended_flat)], axis=1
        ),
        SEQ,
    ).astype(jnp.bfloat16)
    query_grad = summed_grads[:, :query_cols]
    key_grad = summed_grads[:, query_cols : query_cols + kv_cols]
    value_grad = summed_grads[:, query_cols + kv_cols : query_cols + 2 * kv_cols]
    output_grad = summed_grads[:, query_cols + 2 * kv_cols :]
    return (
        passed,
        query_grad[None],
        key_grad[None],
        value_grad[None],
        output_grad[None],
        gain_total[None],
    )


def solution(mesh):
    split = Mesh(
        mesh.devices.reshape(mesh.shape["section"], 8, 2, mesh.shape["tp"]),
        ("section", "seq_0", "seq_1", "tp"),
    )
    placed = (
        P("section", SEQ, None),
        P("section", SEQ, None),
        P("section", None),
        P("section", SEQ, "tp"),
        P("section", SEQ, "tp"),
        P("section", SEQ, "tp"),
        P("section", SEQ, "tp"),
    )
    return jax.shard_map(
        per_device,
        mesh=split,
        in_specs=placed,
        out_specs=(
            P("section", SEQ, None),
            P("section", SEQ, "tp"),
            P("section", SEQ, "tp"),
            P("section", SEQ, "tp"),
            P("section", SEQ, "tp"),
            P("section", "tp"),
        ),
        check_vma=False,
    )
```

profile of v0, /device:TPU:1, one launch (start us, length us, event | category | flops | bytes accessed | tf_op | source)
XLA Modules:
  0.0 458.9 jit_solution(1484858677534150680)
XLA Ops:
  7.2 1.9 pad_maximum_fusion.1
  10.0 2.1 fusion.8
  12.1 142.2 %all-gather.3.cloned.1.call-done = bf16[1,4096,768]{2,1,0:T(8,128)(2,1)} async-done(((bf16[1,256,768]{2,1,0:T(8,128)(2,1)}), bf16[1,4096,768]{2,1,0:T(8,128)(2,1)}) %all-gather.3.cloned.1.call-update) | async-done | bytes 6291472 | tf_op jit(solution)/shard_map/all_gather | solution.py:19
  154.3 2.2 fusion.34
  156.8 2.2 fusion.40
  160.3 3.0 slice_bitcast_fusion.2
  163.3 4.1 copy.44
  167.5 2.6 fusion.18
  170.1 2.4 fusion.31
  172.5 60.8 %all-gather.5.cloned.1.call-done = bf16[4096,2,128]{0,2,1:T(8,128)(2,1)} async-done(((bf16[256,2,128]{0,2,1:T(8,128)(2,1)}), bf16[4096,2,128]{0,2,1:T(8,128)(2,1)}) %all-gather.5.cloned.1.call-update) | async-done | bytes 2097168 | tf_op jit(solution)/shard_map/all_gather | solution.py:19
  233.4 1.7 fusion.130
  244.1 1.4 collective-permute-start
  245.5 1.3 collective-permute-start.7
  246.8 1.3 collective-permute-start.6
  248.1 1.3 collective-permute-start.5
  249.4 1.3 collective-permute-start.4
  251.5 1.3 collective-permute-start.3
  252.8 1.7 collective-permute-done.7
  254.5 1.3 collective-permute-start.2
  255.8 1.3 collective-permute-start.1
  257.1 1.3 collective-permute-start.8
  258.4 1.3 collective-permute-start.15
  259.8 1.3 collective-permute-start.14
  261.1 1.3 collective-permute-start.13
  263.1 1.3 collective-permute-start.12
  264.5 1.3 collective-permute-start.11
  265.8 5.5 %collective-permute-done.15 = bf16[256,1,128]{0,2,1:T(8,128)(2,1)S(1)} collective-permute-done((bf16[256,1,128]{0,2,1:T(8,128)(2,1)S(1)}, bf16[256,1,128]{0,2,1:T(8,128)(2,1)S(1)}, u32[]{:S(2)}, u32[]{:S(2)}) %collective-permute-start.15) | collective-permute-done | bytes 65568 | tf_op jit(solution)/shard_map/ppermute | solution.py:29
  272.5 2.8 collective-permute-done.14
  275.4 1.5 collective-permute-start.9
  277.2 1.5 collective-permute-done.10
  278.7 6.3 %collective-permute-done.9 = bf16[256,1,128]{0,2,1:T(8,128)(2,1)S(1)} collective-permute-done((bf16[256,1,128]{0,2,1:T(8,128)(2,1)S(1)}, bf16[256,1,128]{0,2,1:T(8,128)(2,1)S(1)}, u32[]{:S(2)}, u32[]{:S(2)}) %collective-permute-start.9) | collective-permute-done | bytes 65568 | tf_op jit(solution)/shard_map/ppermute | solution.py:29
  285.1 1.4 convolution_convert_fusion
  286.5 3.4 pad_maximum_fusion
  289.9 2.0 fusion.43
  291.9 2.4 convolution_add_fusion
  294.3 2.0 fusion
  296.3 1.5 copy.58
  297.8 18.7 %all-to-all-start = ((bf16[8,256,512]{2,1,0:T(8,128)(2,1)}), bf16[8,256,512]{2,1,0:T(8,128)(2,1)}, u32[]{:S(2)}, u32[]{:S(2)}) async-start(bf16[8,256,512]{2,1,0:T(8,128)(2,1)} %bitcast.241), calls=%async_computation | async-start | bytes 4194304 | tf_op jit(solution)/shard_map/all_to_all | solution.py:39
  316.5 2.5 convert_element_type.233
  318.9 23.8 %all-to-all-done = bf16[8,256,512]{2,1,0:T(8,128)(2,1)} async-done(((bf16[8,256,512]{2,1,0:T(8,128)(2,1)}), bf16[8,256,512]{2,1,0:T(8,128)(2,1)}, u32[]{:S(2)}, u32[]{:S(2)}) %all-to-all-start) | async-done | bytes 2097184 | tf_op jit(solution)/shard_map/all_to_all | solution.py:39
  342.8 2.0 convert_reduce_fusion
  346.0 8.0 %all_to_all.21 = f32[8,256,1]{1,2,0:T(1,128)S(1)} all-to-all(f32[8,256,1]{1,2,0:T(1,128)S(1)} %broadcast_in_dim.22), channel_id=1, replica_groups=mesh['section'=2,'seq_0'=8,'seq_1'=2,'tp'=8] {'tp'}, dimensions={0} | all-to-all | bytes 16384 | tf_op jit(solution)/shard_map/all_to_all | solution.py:45
  354.1 1.3 fusion.52
  355.6 29.2 %all_to_all.22 = bf16[8,256,512]{2,1,0:T(8,128)(2,1)S(1)} all-to-all(bf16[8,256,512]{2,1,0:T(8,128)(2,1)S(1)} %broadcast_in_dim.23), channel_id=1, replica_groups=mesh['section'=2,'seq_0'=8,'seq_1'=2,'tp'=8] {'tp'}, dimensions={0} | all-to-all | bytes 4194304 | tf_op jit(solution)/shard_map/all_to_all | solution.py:45
  384.8 2.4 copy.47
  387.2 2.6 collective-permute-start.16
  389.8 54.3 %all_to_all.23 = f32[16,1,512]{2,1,0:T(1,128)S(1)} all-to-all(f32[16,1,512]{2,1,0:T(1,128)S(1)} %broadcast_in_dim.28), channel_id=1, replica_groups=mesh['section'=2,'seq_0'=8,'seq_1'=2,'tp'=8] {'seq_0','seq_1'}, dimensions={0} | all-to-all | bytes 65536 | tf_op jit(solution)/shard_map/all_to_all | solution.py:45
  444.7 2.8 copy.49
  (77 shorter events, 21.6 us)
Async XLA Ops:
  7.2 147.1 %copy-start = (bf16[1,256,4096]{2,1,0:T(8,128)(2,1)S(1)}, bf16[1,256,4096]{2,1,0:T(8,128)(2,1)}, u32[]{:S(2)}) copy-start(bf16[1,256,4096]{2,1,0:T(8,128)(2,1)} %param.7) | copy-start | bytes 6291460
  7.2 147.1 %all-gather.3.cloned.1.call-start = ((), (), s32[]{:S(2)}) async-start(), calls=%async_computation.6 | async-start | bytes 6684672 | tf_op jit(solution)/shard_map/all_gather | solution.py:19
  9.2 224.2 %all-gather.5.cloned.1.call-start = ((), (), s32[]{:S(2)}) async-start(), calls=%async_computation.7 | async-start | bytes 2228224 | tf_op jit(solution)/shard_map/all_gather | solution.py:19
  159.7 230.1 %reduce-scatter.3.cloned.1.call-start = ((), (), s32[]{:S(2)}) async-start(), calls=%async_computation.8 | async-start | bytes 7077888 | tf_op jit(solution)/shard_map/reduce_scatter | solution.py:71
  167.5 2.7 copy-start.1
  243.7 7.1 %copy-start.2 = (bf16[1,256,4096]{2,1,0:T(8,128)(2,1)S(1)}, bf16[1,256,4096]{2,1,0:T(8,128)(2,1)}, u32[]{:S(2)}) copy-start(bf16[1,256,4096]{2,1,0:T(8,128)(2,1)} %param.8) | copy-start | bytes 6291460
  244.1 7.4 %collective-permute-start = (bf16[256,1,128]{0,2,1:T(8,128)(2,1)S(1)}, bf16[256,1,128]{0,2,1:T(8,128)(2,1)S(1)}, u32[]{:S(2)}, u32[]{:S(2)}) collective-permute-start(bf16[256,1,128]{0,2,1:T(8,128)(2,1)S(1)} %get-tuple-element.50), channel_id=1, source_target_pairs={{8,0},{16,8},{24,16},{32,24},{40,32},{48,40},{56,48},{64,56},{72,6... | collective-permute-start | bytes 196616 | tf_op jit(solution)/shard_map/ppermute | solution.py:29
  245.5 9.0 %collective-permute-start.7 = (bf16[256,1,128]{0,2,1:T(8,128)(2,1)S(1)}, bf16[256,1,128]{0,2,1:T(8,128)(2,1)S(1)}, u32[]{:S(2)}, u32[]{:S(2)}) collective-permute-start(bf16[256,1,128]{0,2,1:T(8,128)(2,1)S(1)} %get-tuple-element.51), channel_id=1, source_target_pairs={{64,0},{72,8},{80,16},{88,24},{96,32},{104,40},{112,48},{120,56},{... | collective-permute-start | bytes 196616 | tf_op jit(solution)/shard_map/ppermute | solution.py:29
  246.8 9.0 %collective-permute-start.6 = (bf16[256,1,128]{0,2,1:T(8,128)(2,1)S(1)}, bf16[256,1,128]{0,2,1:T(8,128)(2,1)S(1)}, u32[]{:S(2)}, u32[]{:S(2)}) collective-permute-start(bf16[256,1,128]{0,2,1:T(8,128)(2,1)S(1)} %get-tuple-element.52), channel_id=1, source_target_pairs={{56,0},{64,8},{72,16},{80,24},{88,32},{96,40},{104,48},{112,56},{1... | collective-permute-start | bytes 196616 | tf_op jit(solution)/shard_map/ppermute | solution.py:29
  248.1 9.0 %collective-permute-start.5 = (bf16[256,1,128]{0,2,1:T(8,128)(2,1)S(1)}, bf16[256,1,128]{0,2,1:T(8,128)(2,1)S(1)}, u32[]{:S(2)}, u32[]{:S(2)}) collective-permute-start(bf16[256,1,128]{0,2,1:T(8,128)(2,1)S(1)} %get-tuple-element.53), channel_id=1, source_target_pairs={{48,0},{56,8},{64,16},{72,24},{80,32},{88,40},{96,48},{104,56},{11... | collective-permute-start | bytes 196616 | tf_op jit(solution)/shard_map/ppermute | solution.py:29
  249.4 9.0 %collective-permute-start.4 = (bf16[256,1,128]{0,2,1:T(8,128)(2,1)S(1)}, bf16[256,1,128]{0,2,1:T(8,128)(2,1)S(1)}, u32[]{:S(2)}, u32[]{:S(2)}) collective-permute-start(bf16[256,1,128]{0,2,1:T(8,128)(2,1)S(1)} %get-tuple-element.54), channel_id=1, source_target_pairs={{40,0},{48,8},{56,16},{64,24},{72,32},{80,40},{88,48},{96,56},{104... | collective-permute-start | bytes 196616 | tf_op jit(solution)/shard_map/ppermute | solution.py:29
  251.5 8.2 %collective-permute-start.3 = (bf16[256,1,128]{0,2,1:T(8,128)(2,1)S(1)}, bf16[256,1,128]{0,2,1:T(8,128)(2,1)S(1)}, u32[]{:S(2)}, u32[]{:S(2)}) collective-permute-start(bf16[256,1,128]{0,2,1:T(8,128)(2,1)S(1)} %get-tuple-element.55), channel_id=1, source_target_pairs={{32,0},{40,8},{48,16},{56,24},{64,32},{72,40},{80,48},{88,56},{96,... | collective-permute-start | bytes 196616 | tf_op jit(solution)/shard_map/ppermute | solution.py:29
  254.5 6.6 %collective-permute-start.2 = (bf16[256,1,128]{0,2,1:T(8,128)(2,1)S(1)}, bf16[256,1,128]{0,2,1:T(8,128)(2,1)S(1)}, u32[]{:S(2)}, u32[]{:S(2)}) collective-permute-start(bf16[256,1,128]{0,2,1:T(8,128)(2,1)S(1)} %get-tuple-element.56), channel_id=1, source_target_pairs={{24,0},{32,8},{40,16},{48,24},{56,32},{64,40},{72,48},{80,56},{88,... | collective-permute-start | bytes 196616 | tf_op jit(solution)/shard_map/ppermute | solution.py:29
  255.8 7.3 %collective-permute-start.1 = (bf16[256,1,128]{0,2,1:T(8,128)(2,1)S(1)}, bf16[256,1,128]{0,2,1:T(8,128)(2,1)S(1)}, u32[]{:S(2)}, u32[]{:S(2)}) collective-permute-start(bf16[256,1,128]{0,2,1:T(8,128)(2,1)S(1)} %get-tuple-element.57), channel_id=1, source_target_pairs={{16,0},{24,8},{32,16},{40,24},{48,32},{56,40},{64,48},{72,56},{80,... | collective-permute-start | bytes 196616 | tf_op jit(solution)/shard_map/ppermute | solution.py:29
  257.1 7.3 %collective-permute-start.8 = (bf16[256,1,128]{0,2,1:T(8,128)(2,1)S(1)}, bf16[256,1,128]{0,2,1:T(8,128)(2,1)S(1)}, u32[]{:S(2)}, u32[]{:S(2)}) collective-permute-start(bf16[256,1,128]{0,2,1:T(8,128)(2,1)S(1)} %get-tuple-element.42), channel_id=1, source_target_pairs={{8,0},{16,8},{24,16},{32,24},{40,32},{48,40},{56,48},{64,56},{72,6... | collective-permute-start | bytes 196616 | tf_op jit(solution)/shard_map/ppermute | solution.py:29
  258.4 12.8 %collective-permute-start.15 = (bf16[256,1,128]{0,2,1:T(8,128)(2,1)S(1)}, bf16[256,1,128]{0,2,1:T(8,128)(2,1)S(1)}, u32[]{:S(2)}, u32[]{:S(2)}) collective-permute-start(bf16[256,1,128]{0,2,1:T(8,128)(2,1)S(1)} %get-tuple-element.43), channel_id=1, source_target_pairs={{64,0},{72,8},{80,16},{88,24},{96,32},{104,40},{112,48},{120,56},{... | collective-permute-start | bytes 196616 | tf_op jit(solution)/shard_map/ppermute | solution.py:29
  259.8 15.6 %collective-permute-start.14 = (bf16[256,1,128]{0,2,1:T(8,128)(2,1)S(1)}, bf16[256,1,128]{0,2,1:T(8,128)(2,1)S(1)}, u32[]{:S(2)}, u32[]{:S(2)}) collective-permute-start(bf16[256,1,128]{0,2,1:T(8,128)(2,1)S(1)} %get-tuple-element.44), channel_id=1, source_target_pairs={{56,0},{64,8},{72,16},{80,24},{88,32},{96,40},{104,48},{112,56},{1... | collective-permute-start | bytes 196616 | tf_op jit(solution)/shard_map/ppermute | solution.py:29
  261.1 16.1 %collective-permute-start.13 = (bf16[256,1,128]{0,2,1:T(8,128)(2,1)S(1)}, bf16[256,1,128]{0,2,1:T(8,128)(2,1)S(1)}, u32[]{:S(2)}, u32[]{:S(2)}) collective-permute-start(bf16[256,1,128]{0,2,1:T(8,128)(2,1)S(1)} %get-tuple-element.45), channel_id=1, source_target_pairs={{48,0},{56,8},{64,16},{72,24},{80,32},{88,40},{96,48},{104,56},{11... | collective-permute-start | bytes 196616 | tf_op jit(solution)/shard_map/ppermute | solution.py:29
  263.1 14.1 %collective-permute-start.12 = (bf16[256,1,128]{0,2,1:T(8,128)(2,1)S(1)}, bf16[256,1,128]{0,2,1:T(8,128)(2,1)S(1)}, u32[]{:S(2)}, u32[]{:S(2)}) collective-permute-start(bf16[256,1,128]{0,2,1:T(8,128)(2,1)S(1)} %get-tuple-element.46), channel_id=1, source_target_pairs={{40,0},{48,8},{56,16},{64,24},{72,32},{80,40},{88,48},{96,56},{104... | collective-permute-start | bytes 196616 | tf_op jit(solution)/shard_map/ppermute | solution.py:29
  264.5 12.8 %collective-permute-start.11 = (bf16[256,1,128]{0,2,1:T(8,128)(2,1)S(1)}, bf16[256,1,128]{0,2,1:T(8,128)(2,1)S(1)}, u32[]{:S(2)}, u32[]{:S(2)}) collective-permute-start(bf16[256,1,128]{0,2,1:T(8,128)(2,1)S(1)} %get-tuple-element.47), channel_id=1, source_target_pairs={{32,0},{40,8},{48,16},{56,24},{64,32},{72,40},{80,48},{88,56},{96,... | collective-permute-start | bytes 196616 | tf_op jit(solution)/shard_map/ppermute | solution.py:29
  271.2 7.5 %collective-permute-start.10 = (bf16[256,1,128]{0,2,1:T(8,128)(2,1)S(1)}, bf16[256,1,128]{0,2,1:T(8,128)(2,1)S(1)}, u32[]{:S(2)}, u32[]{:S(2)}) collective-permute-start(bf16[256,1,128]{0,2,1:T(8,128)(2,1)S(1)} %get-tuple-element.48), channel_id=1, source_target_pairs={{24,0},{32,8},{40,16},{48,24},{56,32},{64,40},{72,48},{80,56},{88,... | collective-permute-start | bytes 196616 | tf_op jit(solution)/shard_map/ppermute | solution.py:29
  275.4 9.7 %collective-permute-start.9 = (bf16[256,1,128]{0,2,1:T(8,128)(2,1)S(1)}, bf16[256,1,128]{0,2,1:T(8,128)(2,1)S(1)}, u32[]{:S(2)}, u32[]{:S(2)}) collective-permute-start(bf16[256,1,128]{0,2,1:T(8,128)(2,1)S(1)} %get-tuple-element.49), channel_id=1, source_target_pairs={{16,0},{24,8},{32,16},{40,24},{48,32},{56,40},{64,48},{72,56},{80,... | collective-permute-start | bytes 196616 | tf_op jit(solution)/shard_map/ppermute | solution.py:29
  297.8 45.0 %all-to-all-start = ((bf16[8,256,512]{2,1,0:T(8,128)(2,1)}), bf16[8,256,512]{2,1,0:T(8,128)(2,1)}, u32[]{:S(2)}, u32[]{:S(2)}) async-start(bf16[8,256,512]{2,1,0:T(8,128)(2,1)} %bitcast.241), calls=%async_computation | async-start | bytes 4194304 | tf_op jit(solution)/shard_map/all_to_all | solution.py:39
  316.4 131.1 %reduce-scatter.5.cloned.1.call-start = ((), (), s32[]{:S(2)}) async-start(), calls=%async_computation.9 | async-start | bytes 1179648 | tf_op jit(solution)/shard_map/reduce_scatter | solution.py:71
  387.2 57.5 %collective-permute-start.16 = (bf16[1,256,4096]{1,2,0:T(8,128)(2,1)}, bf16[1,256,4096]{1,2,0:T(8,128)(2,1)S(1)}, u32[]{:S(2)}, u32[]{:S(2)}) collective-permute-start(bf16[1,256,4096]{1,2,0:T(8,128)(2,1)} %bitcast.242), channel_id=1, source_target_pairs={{0,128},{128,0},{1,129},{129,1},{2,130},{130,2},{3,131},{131,3},{4... | collective-permute-start | bytes 6291464 | tf_op jit(solution)/shard_map/ppermute | solution.py:65
Sparse Core Ops, SparseCore 0:
  10.3 143.9 all-gather.2
  159.8 73.5 all-gather.4
  290.1 91.4 reduce-scatter.2
  389.9 31.5 reduce-scatter.4
where the time goes:
time: 462 us; the launch traced here: 459 us
  waiting for transfers between devices  245 us (53%)
  blocking collectives  91.5 us (20%)
  starting transfers between devices  42.5 us (9%)
  matrix products  25.1 us (5%)
  local copies, waits for them, and re-layouts  20.7 us (4%)
  other arithmetic  19.3 us (4%)
  between operations  14.3 us (3%)
    all_gather x2, waiting for transfers between devices, in_one_piece(): out, at, done = (lax.all_gather(both, axis, axis=dim, tiled=True), 0, [])  203 us
    all_to_all x3, blocking collectives, sent_to_all(): return lax.all_to_all(copies, axis, split_axis=0, concat_axis=0, tiled=True)  91.5 us
    all_to_all x1, waiting for transfers between devices, summed_on_arrival(): parts = lax.all_to_all(cut_along(shard, dim, count), axis, 0, 0, tiled=True)  23.8 us
    ppermute x16, starting transfers between devices, shifted(): lax.ppermute(value, axis, [(source, source + steps) for source in range(l...  21 us
    all_to_all x1, starting transfers between devices, summed_on_arrival(): parts = lax.all_to_all(cut_along(shard, dim, count), axis, 0, 0, tiled=True)  18.7 us
    ppermute x16, waiting for transfers between devices, shifted(): lax.ppermute(value, axis, [(source, source + steps) for source in range(l...  18.5 us
    dot_general x7, matrix products, contract_last(): lax.dot_general(left_side, right_side, (((1,), (1,)), ((), ())), preferre...  9.59 us
  transfers between devices with their start and end apart: 22, of which 9 were waited for; matrix products, arithmetic and copies ran while one was open for 8% of the time, Pallas kernels for 0%

commit v1 on v0

v1 whole, which is shorter than its diff:
```python
import math

import jax
import jax.numpy as jnp
import numpy as np
from jax import lax
from jax.experimental import pallas as pl
from jax.experimental.pallas import tpu as pltpu
from jax.sharding import Mesh
from jax.sharding import PartitionSpec as P

AXES = ("section", "z", "y", "x", "c")
MESH = pl.DeviceIdType.MESH
D = 4096
HD = 128
WINDOW = 2048
B = 256
NZ = 8
NX = 4
EPS = 1e-05
SCALE = 1.0 / math.sqrt(HD)
F32 = jnp.float32
BF = jnp.bfloat16
RIGHT = (4, 4, 3)
LEFT = (3, 3, 4)


def nt(a, b):
    return lax.dot_general(a, b, (((1,), (1,)), ((), ())), preferred_element_type=F32)


def nn(a, b):
    return lax.dot_general(a, b, (((1,), (0,)), ((), ())), preferred_element_type=F32)


def kernel(
    x_hbm, u_hbm, qw, kw, vw, ow, gain, off_c, off_s, blk_c, blk_s,
    og, gq, gk, gv, go, gg,
    wbuf, xs, xr, xin, invb, isend, irecv, acc, pbuf, rbuf, cosb, sinb,
    qb, kv, dob, qt, dot_, sb, db, mb, lb, oacc, dqa, delta,
    dkve, ysrc, yrcv, zsrc, zrcv, dl, dlt, rds, rdr, rdx, rdy, rdb,
    gs, gr, npo, cs, cr, rss, rsr, nd, ps, gb, gyr,
    l_w, l_x, l_u, l_r,
    w_s, w_r, x_s, x_r, i_s, i_r, p_s, p_r,
    kz_s, ky_s, kv_r, yr_s, yr_r, zr_s, zr_r, d_s, d_r,
    rd_s, rd_r, g_s, g_r, c_s, c_r, n_s, n_r, ps_s, ps_r,
    og_s, og_r, gb_s, gb_r, gy_s, gy_r,
):
    sec = lax.axis_index("section")
    z = lax.axis_index("z")
    y = lax.axis_index("y")
    x = lax.axis_index("x")
    c = lax.axis_index("c")
    s = 2 * z + y
    t = 2 * x + c
    zr_, zl_ = lax.rem(z + 1, NZ), lax.rem(z + NZ - 1, NZ)
    xp, xm, xa = lax.rem(x + 1, NX), lax.rem(x + NX - 1, NX), lax.rem(x + 2, NX)
    py, pc, psec = 1 - y, 1 - c, 1 - sec
    to_y = {"y": py}
    to_c = {"c": pc}
    own = pl.ds(pl.multiple_of(y * B, B), B)
    oth = pl.ds(pl.multiple_of(py * B, B), B)

    def rc(src, dst, ss, rs, dev):
        return pltpu.make_async_remote_copy(
            src_ref=src, dst_ref=dst, send_sem=ss, recv_sem=rs,
            device_id=dev, device_id_type=MESH,
        )

    sends = []

    def send(src, dst, ss, rs, dev):
        copy = rc(src, dst, ss, rs, dev)
        copy.start()
        sends.append(copy)
        return copy

    def arrived(dst, ss, rs, dev):
        rc(dst, dst, ss, rs, dev).wait_recv()

    loads = [
        pltpu.make_async_copy(kw, wbuf.at[z, 0, :, pl.ds(0, HD)], l_w.at[0]),
        pltpu.make_async_copy(vw, wbuf.at[z, 0, :, pl.ds(HD, HD)], l_w.at[1]),
        pltpu.make_async_copy(qw, wbuf.at[z, 1], l_w.at[2]),
        pltpu.make_async_copy(ow, wbuf.at[z, 2], l_w.at[3]),
        pltpu.make_async_copy(x_hbm, xin, l_x),
    ]
    for copy in loads:
        copy.start()

    def cols(blk, parity):
        return pl.ds(pl.multiple_of((2 * blk + parity) * B, B), B)

    for j in range(NZ):
        pltpu.make_async_copy(u_hbm.at[:, cols(j, y)], xs.at[1, j, own, :], l_u).start()
        pltpu.make_async_copy(x_hbm.at[:, cols(j, y)], xr.at[j, own, :], l_r).start()

    barrier = pltpu.get_barrier_semaphore()
    greet = [
        {"z": zr_}, {"z": zl_}, to_y, to_c, {"x": xp}, {"x": xm}, {"x": xa},
        {"section": psec}, {"section": psec, "y": py},
    ]
    for dev in greet:
        pl.semaphore_signal(barrier, inc=1, device_id=dev, device_id_type=MESH)
    pl.semaphore_wait(barrier, len(greet))

    for copy in loads[:4]:
        copy.wait()

    def w_send(h, ch):
        if h < RIGHT[ch]:
            blk = lax.rem(z + NZ - h, NZ)
            send(wbuf.at[blk, ch], wbuf.at[blk, ch], w_s.at[0, h, ch], w_r.at[0, h, ch], {"z": zr_})
        if h < LEFT[ch]:
            blk = lax.rem(z + h, NZ)
            send(wbuf.at[blk, ch], wbuf.at[blk, ch], w_s.at[1, h, ch], w_r.at[1, h, ch], {"z": zl_})

    def w_wait(h, ch):
        if h <= RIGHT[ch]:
            blk = lax.rem(z + NZ - h, NZ)
            arrived(wbuf.at[blk, ch], w_s.at[0, h - 1, ch], w_r.at[0, h - 1, ch], {"z": zr_})
        if h <= LEFT[ch]:
            blk = lax.rem(z + h, NZ)
            arrived(wbuf.at[blk, ch], w_s.at[1, h - 1, ch], w_r.at[1, h - 1, ch], {"z": zl_})

    for ch in range(3):
        w_send(0, ch)

    mine = pl.ds(pl.multiple_of(c * 128, 128), 128)
    there = pl.ds(pl.multiple_of(y * B + c * 128, 128), 128)
    from_y = pl.ds(pl.multiple_of(py * B + c * 128, 128), 128)
    from_c = pl.ds(pl.multiple_of(py * B + pc * 128, 128), 128)
    for j in range(NZ):
        rc(x_hbm.at[mine, cols(j, py)], xr.at[j, there, :], x_s.at[0], x_r.at[0], to_y).start()
    for j in range(NZ):
        rc(u_hbm.at[mine, cols(j, py)], xs.at[1, j, there, :], x_s.at[1], x_r.at[1], to_y).start()
    x_out = rc(xr.at[:, from_y, :], xr.at[:, there, :], x_s.at[0], x_r.at[0], to_y)
    u_out = rc(xs.at[1, :, from_y, :], xs.at[1, :, there, :], x_s.at[1], x_r.at[1], to_y)

    lane = lax.broadcasted_iota(jnp.int32, (B, HD), 1)
    cosb[...] = blk_c[s] * off_c[...] - blk_s[s] * off_s[...]
    sin_all = blk_s[s] * off_c[...] + blk_c[s] * off_s[...]
    sinb[...] = jnp.where(lane < HD // 2, -sin_all, sin_all)

    loads[4].wait()
    invb[own, :] = jnp.zeros((B, HD), F32)

    def squares(j, _):
        v = xin[:, pl.ds(pl.multiple_of(j * B, B), B)].astype(F32)
        invb[own, :] += v[:, :HD] * v[:, :HD] + v[:, HD:] * v[:, HD:]
        return 0

    lax.fori_loop(0, D // B, squares, 0)
    mean = jnp.sum(invb[own, :], axis=1, keepdims=True) / D
    inv_own = jnp.broadcast_to(lax.rsqrt(mean + EPS), (B, HD))
    invb[own, :] = inv_own
    isend[...] = jnp.transpose(inv_own)[:8, :]
    send(isend, irecv, i_s, i_r, to_y)

    whole = pltpu.make_async_copy(xs.at[1, :, oth, :], xs.at[1, :, own, :], l_u)
    whole.wait()
    pltpu.make_async_copy(xr.at[:, oth, :], xr.at[:, own, :], l_r).wait()

    def norm_rows(rows):
        def step(j, _):
            inv = invb[rows, :]
            g = gain[2 * j + y]
            v = xr[j, rows, :].astype(F32)
            n = jnp.concatenate([v[:, :HD] * inv, v[:, HD:] * inv], axis=1) * g
            xs[0, j, rows, :] = n.astype(BF)
            return 0

        lax.fori_loop(0, NZ, step, 0)

    norm_rows(own)

    for h in (1, 2, 3):
        for ch in range(3):
            w_wait(h, ch)
            w_send(h, ch)
        if h == 2:
            x_out.wait_recv()
            send(xr.at[:, from_y, :], xr.at[:, from_y, :], x_s.at[2], x_r.at[2], to_c)
            u_out.wait_recv()
            send(xs.at[1, :, from_y, :], xs.at[1, :, from_y, :], x_s.at[3], x_r.at[3], to_c)

    arrived(irecv, i_s, i_r, to_y)
    inv_oth = jnp.transpose(jnp.broadcast_to(irecv[0:1, :], (HD, B)))
    invb[oth, :] = inv_oth
    arrived(xr.at[:, from_c, :], x_s.at[2], x_r.at[2], to_c)
    norm_rows(oth)
    arrived(xs.at[1, :, from_c, :], x_s.at[3], x_r.at[3], to_c)

    acc[...] = jnp.zeros_like(acc)

    def project(blk, ch):
        sel = jnp.where(ch == 2, 1, 0)
        acc[ch] += nn(xs[sel, blk], wbuf[blk, ch])

    def project_most(n, _):
        project(lax.rem(z + 5 + lax.div(n, 3), NZ), lax.rem(n, 3))
        return 0

    lax.fori_loop(0, 21, project_most, 0)
    for ch in range(3):
        w_wait(4, ch)

    def project_last(ch, _):
        project(lax.rem(z + 4, NZ), ch)
        pbuf[ch] = acc[ch, oth, :].astype(BF)
        rc(pbuf.at[ch], rbuf.at[ch], p_s.at[ch], p_r.at[ch], to_y).start()
        return 0

    lax.fori_loop(0, 3, project_last, 0)
    for ch in range(3):
        sends.append(rc(pbuf.at[ch], rbuf.at[ch], p_s.at[ch], p_r.at[ch], to_y))

    def total(ch):
        arrived(rbuf.at[ch], p_s.at[ch], p_r.at[ch], to_y)
        return acc[ch, own, :] + rbuf[ch].astype(F32)

    def rot(v, sign):
        return v * cosb[...] + pltpu.roll(v, HD // 2, 1) * (sign * sinb[...])

    both = total(0)
    kv[0, 0] = rot(both[:, :HD], 1.0).astype(BF)
    kv[0, 1] = both[:, HD:].astype(BF)

    def kz_send(i, k):
        send(kv.at[2 * i, k], kv.at[2 * i + 2, k], kz_s.at[i, k], kv_r.at[2 * i + 2, k], {"z": zr_})

    def ky_copy(i, k):
        return rc(kv.at[2 * i + 2 * y, k], kv.at[2 * i + 1, k], ky_s.at[i, k], kv_r.at[2 * i + 1, k], to_y)

    for k in range(2):
        kz_send(0, k)

    @pl.when(y == 0)
    def _():
        for k in range(2):
            ky_copy(0, k).start()

    both = total(1)
    for h in range(2):
        q = rot(both[:, h * HD : (h + 1) * HD], 1.0)
        qb[h] = q.astype(BF)
        qt[h] = jnp.transpose(q).astype(BF)
    both = total(2)
    for h in range(2):
        v = both[:, h * HD : (h + 1) * HD]
        dob[h] = v.astype(BF)
        dot_[h] = jnp.transpose(v).astype(BF)

    mb[...] = jnp.full(mb.shape, -3e38, F32)
    diff = lax.broadcasted_iota(jnp.int32, (B, B), 1) - lax.broadcasted_iota(jnp.int32, (B, B), 0)

    def scores(d, _):
        top = jnp.where(s >= d, d * B, -2 * WINDOW)
        allowed = (diff <= top) & (diff > d * B - WINDOW)
        for h in range(2):
            sc = jnp.where(allowed, nt(qb[h], kv[d, 0]) * SCALE, -1e30)
            sb[h, d] = sc
            mb[h] = jnp.maximum(mb[h], jnp.maximum(sc[:, :HD], sc[:, HD:]))
            db[h, d] = nt(dob[h], kv[d, 1])
        return 0

    for i in range(4):
        for k in range(2):
            arrived(kv.at[2 * i + 2, k], kz_s.at[i, k], kv_r.at[2 * i + 2, k], {"z": zr_})
            if i < 3:
                kz_send(i + 1, k)

                @pl.when(y == 0)
                def _():
                    ky_copy(i + 1, k).start()

            @pl.when(y == 1)
            def _():
                ky_copy(i, k).start()

    for i in range(4):
        for k in range(2):
            arrived(kv.at[2 * i + 1, k], ky_s.at[i, k], kv_r.at[2 * i + 1, k], to_y)
            sends.append(ky_copy(i, k))
    lax.fori_loop(0, 9, scores, 0)

    for h in range(2):
        m = jnp.broadcast_to(jnp.max(mb[h], axis=1, keepdims=True), (B, HD))
        mb[h] = m
        lb[h] = jnp.zeros((B, HD), F32)

    def exps(d, _):
        for h in range(2):
            m = mb[h]
            e = jnp.exp(sb[h, d] - jnp.concatenate([m, m], axis=1))
            sb[h, d] = e
            lb[h] += e[:, :HD] + e[:, HD:]
        return 0

    lax.fori_loop(0, 9, exps, 0)
    for h in range(2):
        lb[h] = jnp.broadcast_to(1.0 / jnp.sum(lb[h], axis=1, keepdims=True), (B, HD))
        oacc[h] = jnp.zeros((B, HD), F32)
        dqa[h] = jnp.zeros((B, HD), F32)

    def attend(d, _):
        for h in range(2):
            l = lb[h]
            p = sb[h, d] * jnp.concatenate([l, l], axis=1)
            sb[h, d] = p
            oacc[h] += nn(p.astype(BF), kv[d, 1])
        return 0

    lax.fori_loop(0, 9, attend, 0)
    for h in range(2):
        att = oacc[h].astype(BF)
        dl[2, own, pl.ds(h * HD, HD)] = att
        delta[h] = jnp.broadcast_to(
            jnp.sum(att.astype(F32) * dob[h].astype(F32), axis=1, keepdims=True), (B, HD)
        )

    def dl_send(ch):
        send(dl.at[ch, own, :], dl.at[ch, own, :], d_s.at[ch], d_r.at[ch], to_y)

    dl_send(2)

    def slot_grads(d):
        dkt = jnp.zeros((HD, B), F32)
        dvt = jnp.zeros((HD, B), F32)
        for h in range(2):
            p = sb[h, d]
            r = delta[h]
            ds = (p * (db[h, d] - jnp.concatenate([r, r], axis=1)) * SCALE).astype(BF)
            dqa[h] += nn(ds, kv[d, 0])
            dkt = dkt + nn(qt[h], ds)
            dvt = dvt + nn(dot_[h], p.astype(BF))
        return dkt, dvt

    def y_copy(i):
        return rc(ysrc.at[i], yrcv.at[i], yr_s.at[i], yr_r.at[i], to_y)

    def backward(i, _):
        @pl.when(i < 4)
        def _():
            a, b = slot_grads(7 - 2 * i)
            ysrc[3 - i, 0] = a.astype(BF)
            ysrc[3 - i, 1] = b.astype(BF)
            y_copy(3 - i).start()

        a, b = slot_grads(8 - 2 * i)
        dkve[4 - i, 0] = a
        dkve[4 - i, 1] = b
        return 0

    lax.fori_loop(0, 5, backward, 0)

    for h in range(2):
        dl[1, own, pl.ds(h * HD, HD)] = rot(dqa[h], -1.0).astype(BF)
    dl_send(1)

    def from_partner(e):
        i = e // 2 - y
        keep = jnp.where((i >= 0) & (i < 4), 1.0, 0.0)
        return yrcv[jnp.clip(i, 0, 3)].astype(F32) * keep

    for i in range(4):
        e = 8 - 2 * i
        y_copy(3 - i).wait_recv()
        sends.append(y_copy(3 - i))
        part = dkve[e // 2] + from_partner(e)
        if i > 0:
            arrived(zrcv.at[i - 1], zr_s.at[i - 1], zr_r.at[i - 1], {"z": zl_})
            part = part + zrcv[i - 1].astype(F32)
        zsrc[i] = part.astype(BF)
        send(zsrc.at[i], zrcv.at[i], zr_s.at[i], zr_r.at[i], {"z": zl_})
    arrived(zrcv.at[3], zr_s.at[3], zr_r.at[3], {"z": zl_})
    part = dkve[0] + from_partner(0) + zrcv[3].astype(F32)
    dk = jnp.transpose(part[0])
    dv = jnp.transpose(part[1])
    dl[0, own, pl.ds(0, HD)] = rot(dk, -1.0).astype(BF)
    dl[0, own, pl.ds(HD, HD)] = dv.astype(BF)
    dl_send(0)

    rd = dk * kv[0, 0].astype(F32) + dv * kv[0, 1].astype(F32)
    for h in range(2):
        rd = rd + dqa[h] * qb[h].astype(F32)
    rd = jnp.broadcast_to(jnp.sum(rd, axis=1, keepdims=True), (B, HD))
    rds[0] = jnp.transpose(rd)[:8, :]
    send(rds.at[0], rdr, rd_s.at[0], rd_r.at[0], to_c)

    def dlt_make(ch):
        arrived(dl.at[ch, oth, :], d_s.at[ch], d_r.at[ch], to_y)
        dlt[ch] = jnp.transpose(dl[ch].astype(F32)).astype(BF)

    for ch in range(3):
        dlt_make(ch)

    def parts(i, pc_):
        b = 2 * i + pc_
        return nt(dl[0], wbuf[b, 0]) + nt(dl[1], wbuf[b, 1])

    def parts_out(i, _):
        cs[i] = parts(i, pc).astype(BF)
        rc(cs.at[i], cr.at[i], c_s.at[i], c_r.at[i], to_c).start()
        return 0

    lax.fori_loop(0, NX, parts_out, 0)
    for i in range(NX):
        sends.append(rc(cs.at[i], cr.at[i], c_s.at[i], c_r.at[i], to_c))

    def parts_own(i, _):
        npo[i] = parts(i, c)
        return 0

    lax.fori_loop(0, NX, parts_own, 0)

    def g_copy(way, j, ch):
        dev = {"z": jnp.where(way == 0, zr_, zl_)}
        return rc(gs.at[way, j, ch], gr.at[way, j, ch], g_s.at[way, j, ch], g_r.at[way, j, ch], dev)

    def weight_part(blk, ch):
        sel = jnp.where(ch == 2, 1, 0)
        return nn(dlt[ch], xs[sel, blk])

    def w_step(j):
        count = 6 if j < 3 else 3

        def one(n, _):
            if j < 3:
                ch, way = 2 - lax.div(n, 2), lax.rem(n, 2)
                length = jnp.where((ch < 2) == (way == 0), 4, 3)
            else:
                ch = 2 - n
                way = jnp.where(ch < 2, 0, 1)
                length = 4
            step = jnp.where(way == 0, length - j, NZ - (length - j))
            part = weight_part(lax.rem(z + step, NZ), ch)
            if j > 0:
                g_copy(way, j - 1, ch).wait_recv()
                part = part + gr[way, j - 1, ch].astype(F32)
            gs[way, j, ch] = part.astype(BF)
            g_copy(way, j, ch).start()
            return 0

        lax.fori_loop(0, count, one, 0)

    w_step(0)

    for i in range(NX):
        arrived(cr.at[i], c_s.at[i], c_r.at[i], to_c)
    npo[...] += cr[...].astype(F32)
    up, low = pl.ds(0, B), pl.ds(B, B)

    def r_send(way, k):
        dev = {"x": xp} if way == 0 else {"x": xm}
        send(rss.at[way, k], rsr.at[way, k], n_s.at[way, k], n_r.at[way, k], dev)

    def r_wait(way, k):
        arrived(rsr.at[way, k], n_s.at[way, k], n_r.at[way, k], {"x": xp})

    rss[0, 0] = npo[xa, up, :].astype(BF)
    rss[1, 0] = npo[xa, low, :].astype(BF)
    r_send(0, 0)
    r_send(1, 0)
    rss[0, 1] = npo[xp, low, :].astype(BF)
    rss[1, 1] = npo[xm, up, :].astype(BF)
    r_send(0, 1)
    r_send(1, 1)

    arrived(rdr, rd_s.at[0], rd_r.at[0], to_c)
    rds[1] = rds[0] + rdr[...]
    for k, dev in enumerate(({"x": xp}, {"x": xm}, {"x": xa})):
        send(rds.at[1], rdx.at[k], rd_s.at[1 + k], rd_r.at[1 + k], dev)

    r_wait(0, 0)
    rss[0, 2] = (npo[xp, up, :] + rsr[0, 0].astype(F32)).astype(BF)
    r_send(0, 2)
    r_wait(1, 0)
    rss[1, 2] = (npo[xm, low, :] + rsr[1, 0].astype(F32)).astype(BF)
    r_send(1, 2)

    w_step(1)

    for k in range(3):
        arrived(rdx.at[k], rd_s.at[1 + k], rd_r.at[1 + k], {"x": xp})
    rds[2] = rds[1] + rdx[0] + rdx[1] + rdx[2]
    send(rds.at[2], rdy, rd_s.at[4], rd_r.at[4], to_y)
    rdb[own, :] = jnp.transpose(jnp.broadcast_to(rds[2, 0:1, :], (HD, B)))

    r_wait(0, 1)
    r_wait(1, 1)
    r_wait(0, 2)
    r_wait(1, 2)
    nd[up, :] = npo[x, up, :] + rsr[0, 2].astype(F32) + rsr[1, 1].astype(F32)
    nd[low, :] = npo[x, low, :] + rsr[0, 1].astype(F32) + rsr[1, 2].astype(F32)
    arrived(rdy, rd_s.at[4], rd_r.at[4], to_y)
    rdb[oth, :] = jnp.transpose(jnp.broadcast_to(rdy[0:1, :], (HD, B)))

    for hf in range(2):
        cut = pl.ds(hf * HD, HD)
        inv = invb[...]
        v = xr[t, :, cut].astype(F32)
        n = nd[:, cut]
        g = gain[2 * t + y, :, cut]
        out = xs[1, t, :, cut].astype(F32) + inv * g * n - v * (inv * inv) * rdb[...] * (1.0 / D)
        ps[:, cut] = out.astype(BF)
        gpart = jnp.sum(n * v * inv, axis=0, keepdims=True)
        gb[z, :, cut] = jnp.broadcast_to(gpart, (8, HD))
    send(ps.at[own, :], og.at[t, y], ps_s.at[0], ps_r.at[0], {"section": psec})
    send(ps.at[oth, :], og.at[t, y], ps_s.at[1], ps_r.at[1], {"section": psec, "y": py})

    def gb_send(h):
        blk = lax.rem(z + NZ - h, NZ)
        send(gb.at[blk], gb.at[blk], gb_s.at[0, h], gb_r.at[0, h], {"z": zr_})
        if h < 3:
            blk = lax.rem(z + h, NZ)
            send(gb.at[blk], gb.at[blk], gb_s.at[1, h], gb_r.at[1, h], {"z": zl_})

    def gb_wait(h):
        blk = lax.rem(z + NZ - h, NZ)
        arrived(gb.at[blk], gb_s.at[0, h - 1], gb_r.at[0, h - 1], {"z": zr_})
        if h < 4:
            blk = lax.rem(z + h, NZ)
            arrived(gb.at[blk], gb_s.at[1, h - 1], gb_r.at[1, h - 1], {"z": zl_})

    gb_send(0)

    w_step(2)

    gb_wait(1)
    gb_send(1)

    arrived(og.at[t, y], ps_s.at[0], ps_r.at[0], {"section": psec})
    arrived(og.at[t, py], ps_s.at[1], ps_r.at[1], {"section": psec, "y": py})
    tr, tl, ta = 2 * xm + c, 2 * xp + c, 2 * xa + c

    def og_send(blk, lo, n, k, dev):
        send(og.at[blk, pl.ds(lo, n)], og.at[blk, pl.ds(lo, n)], og_s.at[k], og_r.at[k], dev)

    def og_wait(blk, lo, n, k):
        arrived(og.at[blk, pl.ds(lo, n)], og_s.at[k], og_r.at[k], to_c)

    og_send(t, 0, 1, 0, {"x": xp})
    og_send(t, 1, 1, 1, {"x": xm})
    og_send(t, 1, 1, 2, {"x": xp})
    og_send(t, 0, 1, 3, {"x": xm})
    og_send(t, 0, 2, 4, to_c)

    w_step(3)

    gb_wait(2)
    gb_send(2)

    og_wait(tr, 0, 1, 0)
    og_send(tr, 0, 1, 5, {"x": xp})
    og_wait(tl, 1, 1, 1)
    og_send(tl, 1, 1, 6, {"x": xm})
    og_wait(tr, 1, 1, 2)
    og_send(tr, 0, 2, 7, to_c)
    og_wait(tl, 0, 1, 3)
    og_send(tl, 0, 2, 8, to_c)

    gb_wait(3)
    gb_send(3)

    for ch in (2, 1, 0):
        part = weight_part(z, ch)
        for way, last in ((0, RIGHT[ch] - 1), (1, LEFT[ch] - 1)):
            g_copy(way, last, ch).wait_recv()
            part = part + gr[way, last, ch].astype(F32)
        part = jnp.transpose(part).astype(BF)
        if ch == 2:
            go[...] = part
        elif ch == 1:
            gq[...] = part
        else:
            gk[...] = part[:, :HD]
            gv[...] = part[:, HD:]
    for ch in range(3):
        for j in range(RIGHT[ch]):
            sends.append(g_copy(0, j, ch))
        for j in range(LEFT[ch]):
            sends.append(g_copy(1, j, ch))

    og_wait(ta, 0, 1, 5)
    og_send(ta, 0, 1, 9, to_c)
    og_wait(ta, 1, 1, 6)
    og_send(ta, 1, 1, 10, to_c)

    gb_wait(4)
    gsum = gb[0]
    for i in range(1, NZ):
        gsum = gsum + gb[i]
    gg[y] = gsum
    send(gg.at[y], gg.at[y], gy_s, gy_r, to_y)

    sib = 1 - 2 * c
    og_wait(t + sib, 0, 2, 4)
    og_wait(tr + sib, 0, 2, 7)
    og_wait(tl + sib, 0, 2, 8)
    og_wait(ta + sib, 0, 1, 9)
    og_wait(ta + sib, 1, 1, 10)
    arrived(gg.at[py], gy_s, gy_r, to_y)
    for copy in sends:
        copy.wait_send()
    x_out.wait_send()
    u_out.wait_send()


def tables():
    freq = 10000.0 ** (-2.0 * np.arange(HD // 2) / HD)
    freq = np.concatenate([freq, freq])
    off = np.arange(B)[:, None] * freq[None, :]
    blk = (np.arange(16) * B)[:, None, None] * freq[None, None, :]
    return [a.astype(np.float32) for a in (np.cos(off), np.sin(off), np.cos(blk), np.sin(blk))]


def per_device(layer_input, upstream, norm_gain, query_weight, key_weight, value_weight, output_weight):
    gain = norm_gain[0].astype(F32).reshape(16, 1, B)
    dma = pltpu.SemaphoreType.DMA
    vm = pltpu.VMEM
    scratch = [
        vm((NZ, 3, B, B), BF), vm((2, NZ, 2 * B, B), BF), vm((NZ, 2 * B, B), BF), vm((B, D), BF),
        vm((2 * B, HD), F32), vm((8, B), F32), vm((8, B), F32), vm((3, 2 * B, B), F32),
        vm((3, B, B), BF), vm((3, B, B), BF), vm((B, HD), F32), vm((B, HD), F32),
        vm((2, B, HD), BF), vm((9, 2, B, HD), BF), vm((2, B, HD), BF), vm((2, HD, B), BF), vm((2, HD, B), BF),
        vm((2, 9, B, B), F32), vm((2, 9, B, B), F32),
        vm((2, B, HD), F32), vm((2, B, HD), F32), vm((2, B, HD), F32), vm((2, B, HD), F32), vm((2, B, HD), F32),
        vm((5, 2, HD, B), F32), vm((4, 2, HD, B), BF), vm((4, 2, HD, B), BF), vm((4, 2, HD, B), BF), vm((4, 2, HD, B), BF),
        vm((3, 2 * B, B), BF), vm((3, B, 2 * B), BF),
        vm((3, 8, B), F32), vm((8, B), F32), vm((3, 8, B), F32), vm((8, B), F32), vm((2 * B, HD), F32),
        vm((2, 4, 3, B, B), BF), vm((2, 4, 3, B, B), BF),
        vm((NX, 2 * B, B), F32), vm((NX, 2 * B, B), BF), vm((NX, 2 * B, B), BF),
        vm((2, 3, B, B), BF), vm((2, 3, B, B), BF), vm((2 * B, B), F32), vm((2 * B, B), BF),
        vm((NZ, 8, B), F32), vm((8, B), F32),
        dma((4,)), dma, dma, dma,
        dma((2, 4, 3)), dma((2, 4, 3)), dma((4,)), dma((4,)), dma, dma, dma((3,)), dma((3,)),
        dma((4, 2)), dma((4, 2)), dma((9, 2)), dma((4,)), dma((4,)), dma((4,)), dma((4,)), dma((3,)), dma((3,)),
        dma((5,)), dma((5,)), dma((2, 4, 3)), dma((2, 4, 3)), dma((4,)), dma((4,)), dma((2, 3)), dma((2, 3)),
        dma((2,)), dma((2,)),
        dma((11,)), dma((11,)), dma((2, 4)), dma((2, 4)), dma, dma,
    ]
    hbm = pl.BlockSpec(memory_space=pl.ANY)
    vmem = pl.BlockSpec(memory_space=pltpu.VMEM)
    og, gq, gk, gv, go, gg = pl.pallas_call(
        kernel,
        out_shape=[
            jax.ShapeDtypeStruct((8, 2, B, B), BF),
            jax.ShapeDtypeStruct((B, B), BF),
            jax.ShapeDtypeStruct((B, HD), BF),
            jax.ShapeDtypeStruct((B, HD), BF),
            jax.ShapeDtypeStruct((B, B), BF),
            jax.ShapeDtypeStruct((2, 8, B), F32),
        ],
        in_specs=[hbm] * 6 + [vmem] * 5,
        out_specs=[vmem] * 6,
        scratch_shapes=scratch,
        compiler_params=pltpu.CompilerParams(
            collective_id=0, has_side_effects=True, vmem_limit_bytes=60 * 1024 * 1024
        ),
        name="step",
    )(
        layer_input[0], upstream[0], query_weight[0], key_weight[0], value_weight[0], output_weight[0],
        gain, *tables(),
    )
    passed = jnp.transpose(og, (2, 0, 1, 3)).reshape(1, B, D)
    return passed, gq[None], gk[None], gv[None], go[None], gg[:, 0, :].reshape(1, 2 * B)


def solution(mesh):
    split = Mesh(mesh.devices.reshape(2, NZ, 2, NX, 2), AXES)
    seq, tp = ("z", "y"), ("x", "c")
    rows = P("section", seq, None)
    weight = P("section", seq, tp)
    return jax.shard_map(
        per_device,
        mesh=split,
        in_specs=(rows, rows, P("section", None), weight, weight, weight, weight),
        out_specs=(rows, weight, weight, weight, weight, P("section", tp)),
        check_vma=False,
    )
```

time: 462 us -> 160 us (0.35)
  waiting for transfers between devices: 245 us -> 0 us
  Pallas kernels: 0 us -> 147 us
  blocking collectives: 91.5 us -> 0 us
  starting transfers between devices: 42.5 us -> 0 us
  matrix products: 25.1 us -> 0 us
  other arithmetic: 19.3 us -> 1.34 us
  between operations: 14.3 us -> 0.68 us
  local copies, waits for them, and re-layouts: 20.7 us -> 9.6 us
    all_gather x2 -> x0, waiting for transfers between devices: 203 us -> none  [in_one_piece(): out, at, done = (lax.all_gather(both, axis, axis=dim, tiled=True), 0, [])]
    pallas_call x0 -> x1, Pallas kernels: none -> 147 us  [per_device(): pl.pallas_call(kernel, out_shape=[jax.ShapeDtypeStruct((8, 2, B, B), BF),...]
    all_to_all x3 -> x0, blocking collectives: 91.5 us -> none  [sent_to_all(): return lax.all_to_all(copies, axis, split_axis=0, concat_axis=0, tiled=True)]
    dot_general x21 -> x0, matrix products: 25.1 us -> none  [the longest x7 9.59 us: contract_last(): lax.dot_general(left_side, right_side, (((1,), (1,)), ((), ())), preferre...]
    all_to_all x1 -> x0, waiting for transfers between devices: 23.8 us -> none  [summed_on_arrival(): parts = lax.all_to_all(cut_along(shard, dim, count), axis, 0, 0, tiled=True)]
    ppermute x17 -> x0, starting transfers between devices: 23.5 us -> none  [the longest x16 21 us: shifted(): lax.ppermute(value, axis, [(source, source + steps) for source in range(l...]
    all_to_all x1 -> x0, starting transfers between devices: 18.7 us -> none  [summed_on_arrival(): parts = lax.all_to_all(cut_along(shard, dim, count), axis, 0, 0, tiled=True)]
    ppermute x17 -> x0, waiting for transfers between devices: 18.5 us -> none  [the longest x16 18.5 us: shifted(): lax.ppermute(value, axis, [(source, source + steps) for source in range(l...]
  transfers between devices with their start and end apart: 22 -> 0, of which waited for: 9 -> 0; matrix products, arithmetic and copies ran while one was open for 8% -> 0% of each run, Pallas kernels for 0% -> 0%
where the time goes in v1:
time: 160 us; the launch traced here: 159 us
  Pallas kernels  147 us (92%)
  local copies, waits for them, and re-layouts  9.6 us (6%)
    pallas_call x1, Pallas kernels, per_device(): pl.pallas_call(kernel, out_shape=[jax.ShapeDtypeStruct((8, 2, B, B), BF),...  147 us
    unnamed x13, local copies, waits for them, and re-layouts  5.45 us

profile of v1, /device:TPU:1, one launch (start us, length us, event | category | flops | bytes accessed | tf_op | source)
XLA Modules:
  0.0 158.5 jit_solution(13326007825605575413)
XLA Ops:
  0.6 1.3 convert.1.gain
  2.0 146.9 %step.1 = (bf16[8,2,256,256]{3,2,1,0:T(8,128)(2,1)}, bf16[256,256]{1,0:T(8,128)(2,1)}, bf16[256,128]{1,0:T(8,128)(2,1)}, bf16[256,128]{1,0:T(8,128)(2,1)}, bf16[...) custom-call(bf16[256,4096]{1,0:T(8,128)(2,1)} %bitcast.16, bf16[256,4096]{1,0:T(8,128)(2,1)} %bitcast.17, ...), custom_call_target="tpu_custom_call" | custom-call | tf_op jit(solution)/shard_map/step/pallas_call | solution.py:645
  148.9 2.9 %copy.17 = bf16[256,8,2,256]{0,3,2,1:T(8,128)(2,1)S(1)} copy(bf16[256,8,2,256]{3,0,2,1:T(8,128)(2,1)} %bitcast.18) | data formatting | bytes 4194304 | tf_op jit(solution)/shard_map/transpose | solution.py:666
  151.8 0.0 copy-start.1
  151.8 0.0 copy-start.3
  151.8 0.0 copy-start.2
  151.8 0.0 copy-start
  151.8 2.9 %copy.18 = bf16[1,256,4096]{2,1,0:T(8,128)(2,1)} copy(bf16[1,256,4096]{1,2,0:T(8,128)(2,1)S(1)} %bitcast.15) | data formatting | bytes 4194304
  154.7 1.3 slice.3
  156.0 0.0 copy-done.1
  156.0 0.7 copy.23
  156.6 0.0 copy-done.3
  156.6 0.6 copy.24
  157.3 0.0 copy-done.2
  157.3 0.6 copy.25
  157.9 0.0 copy-done
  157.9 0.7 copy.26
Async XLA Ops:
  151.8 4.2 %copy-start.1 = (bf16[256,256]{1,0:T(8,128)(2,1)S(1)}, bf16[256,256]{1,0:T(8,128)(2,1)}, u32[]{:S(2)}) copy-start(bf16[256,256]{1,0:T(8,128)(2,1)} %get-tuple-element.13) | copy-start | bytes 393220
  151.8 4.8 %copy-start.3 = (bf16[256,128]{1,0:T(8,128)(2,1)S(1)}, bf16[256,128]{1,0:T(8,128)(2,1)}, u32[]{:S(2)}) copy-start(bf16[256,128]{1,0:T(8,128)(2,1)} %get-tuple-element.14) | copy-start | bytes 196612
  151.8 5.5 %copy-start.2 = (bf16[256,128]{1,0:T(8,128)(2,1)S(1)}, bf16[256,128]{1,0:T(8,128)(2,1)}, u32[]{:S(2)}) copy-start(bf16[256,128]{1,0:T(8,128)(2,1)} %get-tuple-element.15) | copy-start | bytes 196612
  151.8 6.1 %copy-start = (bf16[256,256]{1,0:T(8,128)(2,1)S(1)}, bf16[256,256]{1,0:T(8,128)(2,1)}, u32[]{:S(2)}) copy-start(bf16[256,256]{1,0:T(8,128)(2,1)} %get-tuple-element.16) | copy-start | bytes 393220

commit v2 on v1

--- a/solution.py
+++ b/solution.py
@@ -36,10 +36,10 @@
 def kernel(
     x_hbm, u_hbm, qw, kw, vw, ow, gain, off_c, off_s, blk_c, blk_s,
     og, gq, gk, gv, go, gg,
-    wbuf, xs, xr, xin, invb, isend, irecv, acc, pbuf, rbuf, cosb, sinb,
+    gainf, rel, wbuf, xs, xr, xin, invb, isend, irecv, acc, pbuf, rbuf, cosb, sinb,
     qb, kv, dob, qt, dot_, sb, db, mb, lb, oacc, dqa, delta,
     dkve, ysrc, yrcv, zsrc, zrcv, dl, dlt, rds, rdr, rdx, rdy, rdb,
-    gs, gr, npo, cs, cr, rss, rsr, nd, ps, gb, gyr,
+    gs, gr, npart, cs, cr, rss, rsr, nd, ps, gb,
     l_w, l_x, l_u, l_r,
     w_s, w_r, x_s, x_r, i_s, i_r, p_s, p_r,
     kz_s, ky_s, kv_r, yr_s, yr_r, zr_s, zr_r, d_s, d_r,
@@ -98,7 +98,7 @@
     barrier = pltpu.get_barrier_semaphore()
     greet = [
         {"z": zr_}, {"z": zl_}, to_y, to_c, {"x": xp}, {"x": xm}, {"x": xa},
-        {"section": psec}, {"section": psec, "y": py},
+        {"section": psec, "y": py},
     ]
     for dev in greet:
         pl.semaphore_signal(barrier, inc=1, device_id=dev, device_id_type=MESH)
@@ -137,6 +137,9 @@
     x_out = rc(xr.at[:, from_y, :], xr.at[:, there, :], x_s.at[0], x_r.at[0], to_y)
     u_out = rc(xs.at[1, :, from_y, :], xs.at[1, :, there, :], x_s.at[1], x_r.at[1], to_y)
 
+    for j in range(D // B):
+        gainf[j] = gain[:, j * B : (j + 1) * B].astype(F32)
+
     lane = lax.broadcasted_iota(jnp.int32, (B, HD), 1)
     cosb[...] = blk_c[s] * off_c[...] - blk_s[s] * off_s[...]
     sin_all = blk_s[s] * off_c[...] + blk_c[s] * off_s[...]
@@ -164,7 +167,7 @@
     def norm_rows(rows):
         def step(j, _):
             inv = invb[rows, :]
-            g = gain[2 * j + y]
+            g = gainf[2 * j + y]
             v = xr[j, rows, :].astype(F32)
             n = jnp.concatenate([v[:, :HD] * inv, v[:, HD:] * inv], axis=1) * g
             xs[0, j, rows, :] = n.astype(BF)
@@ -339,40 +342,80 @@
     def y_copy(i):
         return rc(ysrc.at[i], yrcv.at[i], yr_s.at[i], yr_r.at[i], to_y)
 
-    def backward(i, _):
-        @pl.when(i < 4)
-        def _():
-            a, b = slot_grads(7 - 2 * i)
-            ysrc[3 - i, 0] = a.astype(BF)
-            ysrc[3 - i, 1] = b.astype(BF)
-            y_copy(3 - i).start()
-
-        a, b = slot_grads(8 - 2 * i)
-        dkve[4 - i, 0] = a
-        dkve[4 - i, 1] = b
-        return 0
-
-    lax.fori_loop(0, 5, backward, 0)
-
-    for h in range(2):
-        dl[1, own, pl.ds(h * HD, HD)] = rot(dqa[h], -1.0).astype(BF)
-    dl_send(1)
+    def slot_pair(i):
+        a, b = slot_grads(2 * i + 1)
+        ysrc[i, 0] = a.astype(BF)
+        ysrc[i, 1] = b.astype(BF)
+        y_copy(i).start()
+        sends.append(y_copy(i))
+        a, b = slot_grads(2 * i + 2)
+        dkve[i + 1, 0] = a
+        dkve[i + 1, 1] = b
 
     def from_partner(e):
         i = e // 2 - y
         keep = jnp.where((i >= 0) & (i < 4), 1.0, 0.0)
         return yrcv[jnp.clip(i, 0, 3)].astype(F32) * keep
 
-    for i in range(4):
+    def chain(i):
         e = 8 - 2 * i
         y_copy(3 - i).wait_recv()
-        sends.append(y_copy(3 - i))
         part = dkve[e // 2] + from_partner(e)
         if i > 0:
             arrived(zrcv.at[i - 1], zr_s.at[i - 1], zr_r.at[i - 1], {"z": zl_})
             part = part + zrcv[i - 1].astype(F32)
         zsrc[i] = part.astype(BF)
         send(zsrc.at[i], zrcv.at[i], zr_s.at[i], zr_r.at[i], {"z": zl_})
+
+    def dlt_make(ch):
+        dlt[ch] = jnp.transpose(dl[ch].astype(F32)).astype(BF)
+
+    def g_copy(way, j, ch):
+        dev = {"z": zr_ if way == 0 else zl_}
+        return rc(gs.at[way, j, ch], gr.at[way, j, ch], g_s.at[way, j, ch], g_r.at[way, j, ch], dev)
+
+    def weight_part(blk, ch):
+        return nn(dlt[ch], xs[1 if ch == 2 else 0, blk])
+
+    def g(way, j, ch):
+        step = 4 - j if way == 0 else NZ - (3 - j)
+        part = weight_part(lax.rem(z + step, NZ), ch)
+        if j > 0:
+            g_copy(way, j - 1, ch).wait_recv()
+            part = part + gr[way, j - 1, ch].astype(F32)
+        gs[way, j, ch] = part.astype(BF)
+        copy = g_copy(way, j, ch)
+        copy.start()
+        sends.append(copy)
+
+    slot_pair(3)
+    slot_pair(2)
+    chain(0)
+    slot_pair(1)
+    chain(1)
+    slot_pair(0)
+    a, b = slot_grads(0)
+    dkve[0, 0] = a
+    dkve[0, 1] = b
+    for h in range(2):
+        dl[1, own, pl.ds(h * HD, HD)] = rot(dqa[h], -1.0).astype(BF)
+    dl_send(1)
+    chain(2)
+    arrived(dl.at[2, oth, :], d_s.at[2], d_r.at[2], to_y)
+    dlt_make(2)
+    g(0, 0, 2)
+    chain(3)
+    arrived(dl.at[1, oth, :], d_s.at[1], d_r.at[1], to_y)
+    dlt_make(1)
+    g(0, 0, 1)
+    g(0, 1, 2)
+
+    def query_parts(b, _):
+        npart[b] = nt(dl[1], wbuf[b, 1])
+        return 0
+
+    lax.fori_loop(0, NZ, query_parts, 0)
+
     arrived(zrcv.at[3], zr_s.at[3], zr_r.at[3], {"z": zl_})
     part = dkve[0] + from_partner(0) + zrcv[3].astype(F32)
     dk = jnp.transpose(part[0])
@@ -388,126 +431,110 @@
     rds[0] = jnp.transpose(rd)[:8, :]
     send(rds.at[0], rdr, rd_s.at[0], rd_r.at[0], to_c)
 
-    def dlt_make(ch):
-        arrived(dl.at[ch, oth, :], d_s.at[ch], d_r.at[ch], to_y)
-        dlt[ch] = jnp.transpose(dl[ch].astype(F32)).astype(BF)
-
-    for ch in range(3):
-        dlt_make(ch)
-
-    def parts(i, pc_):
-        b = 2 * i + pc_
-        return nt(dl[0], wbuf[b, 0]) + nt(dl[1], wbuf[b, 1])
-
-    def parts_out(i, _):
-        cs[i] = parts(i, pc).astype(BF)
-        rc(cs.at[i], cr.at[i], c_s.at[i], c_r.at[i], to_c).start()
-        return 0
-
-    lax.fori_loop(0, NX, parts_out, 0)
-    for i in range(NX):
-        sends.append(rc(cs.at[i], cr.at[i], c_s.at[i], c_r.at[i], to_c))
-
-    def parts_own(i, _):
-        npo[i] = parts(i, c)
-        return 0
-
-    lax.fori_loop(0, NX, parts_own, 0)
-
-    def g_copy(way, j, ch):
-        dev = {"z": jnp.where(way == 0, zr_, zl_)}
-        return rc(gs.at[way, j, ch], gr.at[way, j, ch], g_s.at[way, j, ch], g_r.at[way, j, ch], dev)
-
-    def weight_part(blk, ch):
-        sel = jnp.where(ch == 2, 1, 0)
-        return nn(dlt[ch], xs[sel, blk])
-
-    def w_step(j):
-        count = 6 if j < 3 else 3
-
-        def one(n, _):
-            if j < 3:
-                ch, way = 2 - lax.div(n, 2), lax.rem(n, 2)
-                length = jnp.where((ch < 2) == (way == 0), 4, 3)
-            else:
-                ch = 2 - n
-                way = jnp.where(ch < 2, 0, 1)
-                length = 4
-            step = jnp.where(way == 0, length - j, NZ - (length - j))
-            part = weight_part(lax.rem(z + step, NZ), ch)
-            if j > 0:
-                g_copy(way, j - 1, ch).wait_recv()
-                part = part + gr[way, j - 1, ch].astype(F32)
-            gs[way, j, ch] = part.astype(BF)
-            g_copy(way, j, ch).start()
+    def c_copy(k, i, rows):
+        return rc(cs.at[i, rows, :], cr.at[i, rows, :], c_s.at[k, i], c_r.at[k, i], to_c)
+
+    def parts(k, rows):
+        def out(i, _):
+            b = 2 * i + pc
+            cs[i, rows, :] = (npart[b, rows, :] + nt(dl[0, rows, :], wbuf[b, 0])).astype(BF)
+            c_copy(k, i, rows).start()
             return 0
 
-        lax.fori_loop(0, count, one, 0)
-
-    w_step(0)
-
-    for i in range(NX):
-        arrived(cr.at[i], c_s.at[i], c_r.at[i], to_c)
-    npo[...] += cr[...].astype(F32)
-    up, low = pl.ds(0, B), pl.ds(B, B)
-
-    def r_send(way, k):
+        def keep(i, _):
+            b = 2 * i + c
+            npart[b, rows, :] += nt(dl[0, rows, :], wbuf[b, 0])
+            return 0
+
+        lax.fori_loop(0, NX, out, 0)
+        lax.fori_loop(0, NX, keep, 0)
+        for i in range(NX):
+            sends.append(c_copy(k, i, rows))
+
+    def pair_sum(k, rows):
+        for i in range(NX):
+            c_copy(k, i, rows).wait_recv()
+
+        def add(i, _):
+            npart[2 * i + c, rows, :] += cr[i, rows, :].astype(F32)
+            return 0
+
+        lax.fori_loop(0, NX, add, 0)
+
+    def r_send(way, k, blk, rows, add=None):
+        part = npart[2 * blk + c, rows, :]
+        if add is not None:
+            r_wait(way, add)
+            part = part + rsr[way, add].astype(F32)
+        rss[way, k] = part.astype(BF)
         dev = {"x": xp} if way == 0 else {"x": xm}
         send(rss.at[way, k], rsr.at[way, k], n_s.at[way, k], n_r.at[way, k], dev)
 
     def r_wait(way, k):
         arrived(rsr.at[way, k], n_s.at[way, k], n_r.at[way, k], {"x": xp})
 
-    rss[0, 0] = npo[xa, up, :].astype(BF)
-    rss[1, 0] = npo[xa, low, :].astype(BF)
-    r_send(0, 0)
-    r_send(1, 0)
-    rss[0, 1] = npo[xp, low, :].astype(BF)
-    rss[1, 1] = npo[xm, up, :].astype(BF)
-    r_send(0, 1)
-    r_send(1, 1)
-
+    parts(0, own)
+    g(0, 1, 1)
+    pair_sum(0, own)
+    r_send(0, 0, xa, own)
+    r_send(1, 0, xm, own)
     arrived(rdr, rd_s.at[0], rd_r.at[0], to_c)
     rds[1] = rds[0] + rdr[...]
     for k, dev in enumerate(({"x": xp}, {"x": xm}, {"x": xa})):
         send(rds.at[1], rdx.at[k], rd_s.at[1 + k], rd_r.at[1 + k], dev)
-
-    r_wait(0, 0)
-    rss[0, 2] = (npo[xp, up, :] + rsr[0, 0].astype(F32)).astype(BF)
-    r_send(0, 2)
-    r_wait(1, 0)
-    rss[1, 2] = (npo[xm, low, :] + rsr[1, 0].astype(F32)).astype(BF)
-    r_send(1, 2)
-
-    w_step(1)
-
+    g(1, 0, 2)
+    g(1, 0, 1)
+    g(0, 2, 2)
+
+    arrived(dl.at[0, oth, :], d_s.at[0], d_r.at[0], to_y)
+    parts(1, oth)
+    pair_sum(1, oth)
+    r_send(1, 1, xa, oth)
+    r_send(0, 1, xp, own, 0)
+    r_send(0, 2, xp, oth)
+
+    dlt_make(0)
+    g(0, 0, 0)
+    g(1, 0, 0)
+    g(0, 2, 1)
+    g(1, 1, 2)
+    g(1, 1, 1)
     for k in range(3):
         arrived(rdx.at[k], rd_s.at[1 + k], rd_r.at[1 + k], {"x": xp})
     rds[2] = rds[1] + rdx[0] + rdx[1] + rdx[2]
     send(rds.at[2], rdy, rd_s.at[4], rd_r.at[4], to_y)
     rdb[own, :] = jnp.transpose(jnp.broadcast_to(rds[2, 0:1, :], (HD, B)))
-
-    r_wait(0, 1)
-    r_wait(1, 1)
-    r_wait(0, 2)
-    r_wait(1, 2)
-    nd[up, :] = npo[x, up, :] + rsr[0, 2].astype(F32) + rsr[1, 1].astype(F32)
-    nd[low, :] = npo[x, low, :] + rsr[0, 1].astype(F32) + rsr[1, 2].astype(F32)
+    r_send(1, 2, xm, oth, 1)
+
+    def share(rows, first, second):
+        r_wait(*first)
+        r_wait(*second)
+        nd[rows, :] = npart[t, rows, :] + rsr[first].astype(F32) + rsr[second].astype(F32)
+        for hf in range(2):
+            cut = pl.ds(hf * HD, HD)
+            inv = invb[rows, :]
+            v = xr[t, rows, cut].astype(F32)
+            n = nd[rows, cut]
+            gn = gainf[2 * t + y, :, cut]
+            out = xs[1, t, rows, cut].astype(F32) + inv * gn * n - v * (inv * inv) * rdb[rows, :] * (1.0 / D)
+            ps[rows, cut] = out.astype(BF)
+
+    def gain_term(rows, cut):
+        return jnp.sum(nd[rows, cut] * xr[t, rows, cut].astype(F32) * invb[rows, :], axis=0, keepdims=True)
+
+    across = {"section": psec, "y": py}
+    share(own, (0, 1), (1, 0))
+    send(ps.at[own, :], rel, ps_s.at[0], ps_r.at[0], across)
+    g(0, 3, 2)
+    g(0, 1, 0)
+    g(1, 1, 0)
     arrived(rdy, rd_s.at[4], rd_r.at[4], to_y)
     rdb[oth, :] = jnp.transpose(jnp.broadcast_to(rdy[0:1, :], (HD, B)))
-
+    share(oth, (0, 2), (1, 2))
+    send(ps.at[oth, :], og.at[t, y], ps_s.at[1], ps_r.at[1], across)
     for hf in range(2):
         cut = pl.ds(hf * HD, HD)
-        inv = invb[...]
-        v = xr[t, :, cut].astype(F32)
-        n = nd[:, cut]
-        g = gain[2 * t + y, :, cut]
-        out = xs[1, t, :, cut].astype(F32) + inv * g * n - v * (inv * inv) * rdb[...] * (1.0 / D)
-        ps[:, cut] = out.astype(BF)
-        gpart = jnp.sum(n * v * inv, axis=0, keepdims=True)
-        gb[z, :, cut] = jnp.broadcast_to(gpart, (8, HD))
-    send(ps.at[own, :], og.at[t, y], ps_s.at[0], ps_r.at[0], {"section": psec})
-    send(ps.at[oth, :], og.at[t, y], ps_s.at[1], ps_r.at[1], {"section": psec, "y": py})
+        gb[z, :, cut] = jnp.broadcast_to(gain_term(own, cut) + gain_term(oth, cut), (8, HD))
 
     def gb_send(h):
         blk = lax.rem(z + NZ - h, NZ)
@@ -524,48 +551,52 @@
             arrived(gb.at[blk], gb_s.at[1, h - 1], gb_r.at[1, h - 1], {"z": zl_})
 
     gb_send(0)
-
-    w_step(2)
-
+    g(0, 3, 1)
+    g(1, 2, 2)
+
+    arrived(rel, ps_s.at[0], ps_r.at[0], across)
+    send(rel, og.at[t, py], ps_s.at[2], ps_r.at[2], to_y)
+    g(1, 2, 1)
+    g(0, 2, 0)
+
+    tr, tl, ta = 2 * xm + c, 2 * xp + c, 2 * xa + c
+
+    def og_send(blk, par, k, dev):
+        send(og.at[blk, par], og.at[blk, par], og_s.at[k], og_r.at[k], dev)
+
+    def og_wait(blk, par, k):
+        arrived(og.at[blk, par], og_s.at[k], og_r.at[k], to_c)
+
+    arrived(og.at[t, py], ps_s.at[1], ps_r.at[1], across)
+    og_send(t, py, 0, {"x": xp})
+    og_send(t, py, 1, {"x": xm})
+    og_send(t, py, 6, to_c)
+    arrived(og.at[t, y], ps_s.at[2], ps_r.at[2], to_y)
+    og_send(t, y, 2, {"x": xp})
+    og_send(t, y, 3, {"x": xm})
+    og_send(t, y, 7, to_c)
     gb_wait(1)
     gb_send(1)
-
-    arrived(og.at[t, y], ps_s.at[0], ps_r.at[0], {"section": psec})
-    arrived(og.at[t, py], ps_s.at[1], ps_r.at[1], {"section": psec, "y": py})
-    tr, tl, ta = 2 * xm + c, 2 * xp + c, 2 * xa + c
-
-    def og_send(blk, lo, n, k, dev):
-        send(og.at[blk, pl.ds(lo, n)], og.at[blk, pl.ds(lo, n)], og_s.at[k], og_r.at[k], dev)
-
-    def og_wait(blk, lo, n, k):
-        arrived(og.at[blk, pl.ds(lo, n)], og_s.at[k], og_r.at[k], to_c)
-
-    og_send(t, 0, 1, 0, {"x": xp})
-    og_send(t, 1, 1, 1, {"x": xm})
-    og_send(t, 1, 1, 2, {"x": xp})
-    og_send(t, 0, 1, 3, {"x": xm})
-    og_send(t, 0, 2, 4, to_c)
-
-    w_step(3)
-
+    g(1, 2, 0)
+    og_wait(tr, py, 0)
+    og_send(tr, py, 4, {"x": xp})
+    og_send(tr, py, 8, to_c)
+    og_wait(tl, py, 1)
+    og_send(tl, py, 9, to_c)
     gb_wait(2)
     gb_send(2)
-
-    og_wait(tr, 0, 1, 0)
-    og_send(tr, 0, 1, 5, {"x": xp})
-    og_wait(tl, 1, 1, 1)
-    og_send(tl, 1, 1, 6, {"x": xm})
-    og_wait(tr, 1, 1, 2)
-    og_send(tr, 0, 2, 7, to_c)
-    og_wait(tl, 0, 1, 3)
-    og_send(tl, 0, 2, 8, to_c)
-
+    og_wait(tl, y, 3)
+    og_send(tl, y, 5, {"x": xm})
+    og_send(tl, y, 11, to_c)
+    og_wait(tr, y, 2)
+    og_send(tr, y, 10, to_c)
+    g(0, 3, 0)
     gb_wait(3)
     gb_send(3)
 
     for ch in (2, 1, 0):
         part = weight_part(z, ch)
-        for way, last in ((0, RIGHT[ch] - 1), (1, LEFT[ch] - 1)):
+        for way, last in ((0, 3), (1, 2)):
             g_copy(way, last, ch).wait_recv()
             part = part + gr[way, last, ch].astype(F32)
         part = jnp.transpose(part).astype(BF)
@@ -576,16 +607,11 @@
         else:
             gk[...] = part[:, :HD]
             gv[...] = part[:, HD:]
-    for ch in range(3):
-        for j in range(RIGHT[ch]):
-            sends.append(g_copy(0, j, ch))
-        for j in range(LEFT[ch]):
-            sends.append(g_copy(1, j, ch))
-
-    og_wait(ta, 0, 1, 5)
-    og_send(ta, 0, 1, 9, to_c)
-    og_wait(ta, 1, 1, 6)
-    og_send(ta, 1, 1, 10, to_c)
+
+    og_wait(ta, py, 4)
+    og_send(ta, py, 12, to_c)
+    og_wait(ta, y, 5)
+    og_send(ta, y, 13, to_c)
 
     gb_wait(4)
     gsum = gb[0]
@@ -595,16 +621,27 @@
     send(gg.at[y], gg.at[y], gy_s, gy_r, to_y)
 
     sib = 1 - 2 * c
-    og_wait(t + sib, 0, 2, 4)
-    og_wait(tr + sib, 0, 2, 7)
-    og_wait(tl + sib, 0, 2, 8)
-    og_wait(ta + sib, 0, 1, 9)
-    og_wait(ta + sib, 1, 1, 10)
+    for blk, ks in ((t, (6, 7)), (tr, (8, 10)), (tl, (9, 11)), (ta, (12, 13))):
+        og_wait(blk + sib, py, ks[0])
+        og_wait(blk + sib, y, ks[1])
     arrived(gg.at[py], gy_s, gy_r, to_y)
     for copy in sends:
         copy.wait_send()
     x_out.wait_send()
     u_out.wait_send()
+
+
+def finish(og, gq, gk, gv, go, gg, passed, oq, ok, ov, oo, gain_sum):
+    for blk in range(8):
+        for par in range(2):
+            at = (2 * blk + par) * B
+            passed[0, :, at : at + B] = og[blk, par]
+    oq[0] = gq[...]
+    ok[0] = gk[...]
+    ov[0] = gv[...]
+    oo[0] = go[...]
+    gain_sum[:, :B] = gg[0, 0:1, :]
+    gain_sum[:, B:] = gg[1, 0:1, :]
 
 
 def tables():
@@ -616,10 +653,10 @@
 
 
 def per_device(layer_input, upstream, norm_gain, query_weight, key_weight, value_weight, output_weight):
-    gain = norm_gain[0].astype(F32).reshape(16, 1, B)
     dma = pltpu.SemaphoreType.DMA
     vm = pltpu.VMEM
     scratch = [
+        vm((D // B, 1, B), F32), vm((B, B), BF),
         vm((NZ, 3, B, B), BF), vm((2, NZ, 2 * B, B), BF), vm((NZ, 2 * B, B), BF), vm((B, D), BF),
         vm((2 * B, HD), F32), vm((8, B), F32), vm((8, B), F32), vm((3, 2 * B, B), F32),
         vm((3, B, B), BF), vm((3, B, B), BF), vm((B, HD), F32), vm((B, HD), F32),
@@ -630,15 +667,15 @@
         vm((3, 2 * B, B), BF), vm((3, B, 2 * B), BF),
         vm((3, 8, B), F32), vm((8, B), F32), vm((3, 8, B), F32), vm((8, B), F32), vm((2 * B, HD), F32),
         vm((2, 4, 3, B, B), BF), vm((2, 4, 3, B, B), BF),
-        vm((NX, 2 * B, B), F32), vm((NX, 2 * B, B), BF), vm((NX, 2 * B, B), BF),
+        vm((NZ, 2 * B, B), F32), vm((NX, 2 * B, B), BF), vm((NX, 2 * B, B), BF),
         vm((2, 3, B, B), BF), vm((2, 3, B, B), BF), vm((2 * B, B), F32), vm((2 * B, B), BF),
-        vm((NZ, 8, B), F32), vm((8, B), F32),
+        vm((NZ, 8, B), F32),
         dma((4,)), dma, dma, dma,
         dma((2, 4, 3)), dma((2, 4, 3)), dma((4,)), dma((4,)), dma, dma, dma((3,)), dma((3,)),
         dma((4, 2)), dma((4, 2)), dma((9, 2)), dma((4,)), dma((4,)), dma((4,)), dma((4,)), dma((3,)), dma((3,)),
-        dma((5,)), dma((5,)), dma((2, 4, 3)), dma((2, 4, 3)), dma((4,)), dma((4,)), dma((2, 3)), dma((2, 3)),
-        dma((2,)), dma((2,)),
-        dma((11,)), dma((11,)), dma((2, 4)), dma((2, 4)), dma, dma,
+        dma((5,)), dma((5,)), dma((2, 4, 3)), dma((2, 4, 3)), dma((2, 4)), dma((2, 4)), dma((2, 3)), dma((2, 3)),
+        dma((3,)), dma((3,)),
+        dma((14,)), dma((14,)), dma((2, 4)), dma((2, 4)), dma, dma,
     ]
     hbm = pl.BlockSpec(memory_space=pl.ANY)
     vmem = pl.BlockSpec(memory_space=pltpu.VMEM)
@@ -661,10 +698,22 @@
         name="step",
     )(
         layer_input[0], upstream[0], query_weight[0], key_weight[0], value_weight[0], output_weight[0],
-        gain, *tables(),
+        norm_gain, *tables(),
     )
-    passed = jnp.transpose(og, (2, 0, 1, 3)).reshape(1, B, D)
-    return passed, gq[None], gk[None], gv[None], go[None], gg[:, 0, :].reshape(1, 2 * B)
+    return pl.pallas_call(
+        finish,
+        out_shape=[
+            jax.ShapeDtypeStruct((1, B, D), BF),
+            jax.ShapeDtypeStruct((1, B, B), BF),
+            jax.ShapeDtypeStruct((1, B, HD), BF),
+            jax.ShapeDtypeStruct((1, B, HD), BF),
+            jax.ShapeDtypeStruct((1, B, B), BF),
+            jax.ShapeDtypeStruct((1, 2 * B), F32),
+        ],
+        in_specs=[vmem] * 6,
+        out_specs=[vmem] * 6,
+        name="finish",
+    )(og, gq, gk, gv, go, gg)
 
 
 def solution(mesh):

time: 160 us -> 146 us (0.912); the launches traced: 159 us -> 146 us
  local copies, waits for them, and re-layouts: 9.6 us -> 0 us
    unnamed x13 -> x0, local copies, waits for them, and re-layouts: 5.45 us -> none
    pallas_call x1, Pallas kernels: 147 us -> 142 us  [per_device(): pl.pallas_call(kernel, out_shape=[jax.ShapeDtypeStruct((8, 2, B, B), BF),...]
    pallas_call x0 -> x1, Pallas kernels: none -> 3.36 us  [per_device(): pl.pallas_call(finish, out_shape=[jax.ShapeDtypeStruct((1, B, D), BF), ja...]
    transpose x1 -> x0, local copies, waits for them, and re-layouts: 2.86 us -> none  [per_device(): passed = jnp.transpose(og, (2, 0, 1, 3)).reshape(1, B, D)]
where the time goes in v2:
time: 146 us
  Pallas kernels  146 us (100%)
    pallas_call x1, Pallas kernels, per_device(): pl.pallas_call(kernel, out_shape=[jax.ShapeDtypeStruct((8, 2, B, B), BF),...  142 us
    pallas_call x1, Pallas kernels, per_device(): pl.pallas_call(finish, out_shape=[jax.ShapeDtypeStruct((1, B, D), BF), ja...  3.36 us

profile of v2, /device:TPU:1, one launch (start us, length us, event | category | flops | bytes accessed | tf_op | source)
XLA Modules:
  0.0 146.2 jit_solution(9023688007359717477)
XLA Ops:
  0.6 142.2 %step.1 = (bf16[8,2,256,256]{3,2,1,0:T(8,128)(2,1)}, bf16[256,256]{1,0:T(8,128)(2,1)}, bf16[256,128]{1,0:T(8,128)(2,1)}, bf16[256,128]{1,0:T(8,128)(2,1)}, bf16[...) custom-call(bf16[256,4096]{1,0:T(8,128)(2,1)} %bitcast.6, bf16[256,4096]{1,0:T(8,128)(2,1)} %bitcast.7, ...), custom_call_target="tpu_custom_call" | custom-call | tf_op jit(solution)/shard_map/step/pallas_call | solution.py:682
  142.9 3.4 %finish.1 = (bf16[1,256,4096]{2,1,0:T(8,128)(2,1)}, bf16[1,256,256]{2,1,0:T(8,128)(2,1)}, bf16[1,256,128]{2,1,0:T(8,128)(2,1)}, bf16[1,256,128]{2,1,0:T(8,128)(2...) custom-call(bf16[8,2,256,256]{3,2,1,0:T(8,128)(2,1)} %get-tuple-element.12.og, ...), custom_call_target="tpu_custom_call" | custom-call | tf_op jit(solution)/shard_map/finish/pallas_call | solution.py:703

commit v3 on v2

--- a/solution.py
+++ b/solution.py
@@ -21,8 +21,8 @@
 SCALE = 1.0 / math.sqrt(HD)
 F32 = jnp.float32
 BF = jnp.bfloat16
-RIGHT = (4, 4, 3)
-LEFT = (3, 3, 4)
+RIGHT = (4, 3, 4, 3, 4, 3)
+LEFT = (3, 4, 3, 4, 3, 4)
 
 
 def nt(a, b):
@@ -37,7 +37,7 @@
     x_hbm, u_hbm, qw, kw, vw, ow, gain, off_c, off_s, blk_c, blk_s,
     og, gq, gk, gv, go, gg,
     gainf, rel, wbuf, xs, xr, xin, invb, isend, irecv, acc, pbuf, rbuf, cosb, sinb,
-    qb, kv, dob, qt, dot_, sb, db, mb, lb, oacc, dqa, delta,
+    qb, kv, dob, qt, dot_, sb, db, msl, mb, lb, oacc, dqa, delta,
     dkve, ysrc, yrcv, zsrc, zrcv, dl, dlt, rds, rdr, rdx, rdy, rdb,
     gs, gr, npart, cs, cr, rss, rsr, nd, ps, gb,
     l_w, l_x, l_u, l_r,
@@ -107,24 +107,35 @@
     for copy in loads[:4]:
         copy.wait()
 
-    def w_send(h, ch):
-        if h < RIGHT[ch]:
-            blk = lax.rem(z + NZ - h, NZ)
-            send(wbuf.at[blk, ch], wbuf.at[blk, ch], w_s.at[0, h, ch], w_r.at[0, h, ch], {"z": zr_})
-        if h < LEFT[ch]:
-            blk = lax.rem(z + h, NZ)
-            send(wbuf.at[blk, ch], wbuf.at[blk, ch], w_s.at[1, h, ch], w_r.at[1, h, ch], {"z": zl_})
-
-    def w_wait(h, ch):
-        if h <= RIGHT[ch]:
-            blk = lax.rem(z + NZ - h, NZ)
-            arrived(wbuf.at[blk, ch], w_s.at[0, h - 1, ch], w_r.at[0, h - 1, ch], {"z": zr_})
-        if h <= LEFT[ch]:
-            blk = lax.rem(z + h, NZ)
-            arrived(wbuf.at[blk, ch], w_s.at[1, h - 1, ch], w_r.at[1, h - 1, ch], {"z": zl_})
-
-    for ch in range(3):
-        w_send(0, ch)
+    def w_half(blk, n):
+        return wbuf.at[blk, n // 2, :, pl.ds(n % 2 * HD, HD)]
+
+    def w_copy(way, h, n):
+        blk = lax.rem(z + NZ - h, NZ) if way == 0 else lax.rem(z + h, NZ)
+        dev = {"z": zr_ if way == 0 else zl_}
+        return rc(w_half(blk, n), w_half(blk, n), w_s.at[way, h, n], w_r.at[way, h, n], dev)
+
+    def w_send(h, n):
+        for way, hops in ((0, RIGHT), (1, LEFT)):
+            if h < hops[n]:
+                copy = w_copy(way, h, n)
+                copy.start()
+                sends.append(copy)
+
+    def w_wait(h, n):
+        for way, hops in ((0, RIGHT), (1, LEFT)):
+            if h <= hops[n]:
+                blk = lax.rem(z + NZ - h, NZ) if way == 0 else lax.rem(z + h, NZ)
+                arrived(w_half(blk, n), w_s.at[way, h - 1, n], w_r.at[way, h - 1, n], {"z": zr_})
+
+    def w_hop(h, halves):
+        for n in halves:
+            w_wait(h, n)
+            w_send(h, n)
+
+    early, late = (0, 1, 2), (3, 4, 5)
+    for n in early:
+        w_send(0, n)
 
     mine = pl.ds(pl.multiple_of(c * 128, 128), 128)
     there = pl.ds(pl.multiple_of(y * B + c * 128, 128), 128)
@@ -132,10 +143,24 @@
     from_c = pl.ds(pl.multiple_of(py * B + pc * 128, 128), 128)
     for j in range(NZ):
         rc(x_hbm.at[mine, cols(j, py)], xr.at[j, there, :], x_s.at[0], x_r.at[0], to_y).start()
-    for j in range(NZ):
-        rc(u_hbm.at[mine, cols(j, py)], xs.at[1, j, there, :], x_s.at[1], x_r.at[1], to_y).start()
+
+    def u_start(part):
+        for j in range(4 * part, 4 * part + 4):
+            dst = xs.at[1, j, there, :]
+            rc(u_hbm.at[mine, cols(j, py)], dst, x_s.at[1 + part], x_r.at[1 + part], to_y).start()
+
+    def u_rows(part, rows):
+        return xs.at[1, pl.ds(4 * part, 4), rows, :]
+
+    u_start(0)
     x_out = rc(xr.at[:, from_y, :], xr.at[:, there, :], x_s.at[0], x_r.at[0], to_y)
-    u_out = rc(xs.at[1, :, from_y, :], xs.at[1, :, there, :], x_s.at[1], x_r.at[1], to_y)
+    u_out = [
+        rc(u_rows(p, from_y), u_rows(p, there), x_s.at[1 + p], x_r.at[1 + p], to_y) for p in range(2)
+    ]
+
+    def u_take(part):
+        u_out[part].wait_recv()
+        send(u_rows(part, from_y), u_rows(part, from_y), x_s.at[4 + part], x_r.at[4 + part], to_c)
 
     for j in range(D // B):
         gainf[j] = gain[:, j * B : (j + 1) * B].astype(F32)
@@ -178,53 +203,51 @@
     norm_rows(own)
 
     for h in (1, 2, 3):
-        for ch in range(3):
-            w_wait(h, ch)
-            w_send(h, ch)
-        if h == 2:
-            x_out.wait_recv()
-            send(xr.at[:, from_y, :], xr.at[:, from_y, :], x_s.at[2], x_r.at[2], to_c)
-            u_out.wait_recv()
-            send(xs.at[1, :, from_y, :], xs.at[1, :, from_y, :], x_s.at[3], x_r.at[3], to_c)
+        w_hop(h, early)
+    for n in late:
+        w_send(0, n)
+    x_out.wait_recv()
+    send(xr.at[:, from_y, :], xr.at[:, from_y, :], x_s.at[3], x_r.at[3], to_c)
 
     arrived(irecv, i_s, i_r, to_y)
     inv_oth = jnp.transpose(jnp.broadcast_to(irecv[0:1, :], (HD, B)))
     invb[oth, :] = inv_oth
-    arrived(xr.at[:, from_c, :], x_s.at[2], x_r.at[2], to_c)
+    arrived(xr.at[:, from_c, :], x_s.at[3], x_r.at[3], to_c)
     norm_rows(oth)
-    arrived(xs.at[1, :, from_c, :], x_s.at[3], x_r.at[3], to_c)
-
-    acc[...] = jnp.zeros_like(acc)
-
-    def project(blk, ch):
-        sel = jnp.where(ch == 2, 1, 0)
-        acc[ch] += nn(xs[sel, blk], wbuf[blk, ch])
-
-    def project_most(n, _):
-        project(lax.rem(z + 5 + lax.div(n, 3), NZ), lax.rem(n, 3))
-        return 0
-
-    lax.fori_loop(0, 21, project_most, 0)
-    for ch in range(3):
-        w_wait(4, ch)
-
-    def project_last(ch, _):
-        project(lax.rem(z + 4, NZ), ch)
+
+    def project(ch, lo, hi):
+        def step(n, _):
+            blk = lax.rem(z + 5 + n, NZ)
+            acc[ch] += nn(xs[1 if ch == 2 else 0, blk], wbuf[blk, ch])
+            return 0
+
+        if lo == 0:
+            acc[ch] = jnp.zeros((2 * B, B), F32)
+        lax.fori_loop(lo, hi, step, 0)
+
+    def p_copy(ch):
+        return rc(pbuf.at[ch], rbuf.at[ch], p_s.at[ch], p_r.at[ch], to_y)
+
+    def project_out(ch):
         pbuf[ch] = acc[ch, oth, :].astype(BF)
-        rc(pbuf.at[ch], rbuf.at[ch], p_s.at[ch], p_r.at[ch], to_y).start()
-        return 0
-
-    lax.fori_loop(0, 3, project_last, 0)
-    for ch in range(3):
-        sends.append(rc(pbuf.at[ch], rbuf.at[ch], p_s.at[ch], p_r.at[ch], to_y))
+        p_copy(ch).start()
+        sends.append(p_copy(ch))
 
     def total(ch):
-        arrived(rbuf.at[ch], p_s.at[ch], p_r.at[ch], to_y)
+        p_copy(ch).wait_recv()
         return acc[ch, own, :] + rbuf[ch].astype(F32)
 
     def rot(v, sign):
         return v * cosb[...] + pltpu.roll(v, HD // 2, 1) * (sign * sinb[...])
 
+    project(0, 0, 7)
+    for n in early:
+        w_wait(4, n)
+    project(0, 7, 8)
+    project_out(0)
+    u_start(1)
+    w_hop(1, late)
+    u_take(0)
     both = total(0)
     kv[0, 0] = rot(both[:, :HD], 1.0).astype(BF)
     kv[0, 1] = both[:, HD:].astype(BF)
@@ -235,14 +258,50 @@
     def ky_copy(i, k):
         return rc(kv.at[2 * i + 2 * y, k], kv.at[2 * i + 1, k], ky_s.at[i, k], kv_r.at[2 * i + 1, k], to_y)
 
+    def ky_start(i, k, side):
+        @pl.when(y == side)
+        def _():
+            ky_copy(i, k).start()
+
     for k in range(2):
         kz_send(0, k)
-
-    @pl.when(y == 0)
-    def _():
+        ky_start(0, k, 0)
+
+    def halo(i):
         for k in range(2):
-            ky_copy(0, k).start()
-
+            arrived(kv.at[2 * i + 2, k], kz_s.at[i, k], kv_r.at[2 * i + 2, k], {"z": zr_})
+            if i < 3:
+                kz_send(i + 1, k)
+                ky_start(i + 1, k, 0)
+            ky_start(i, k, 1)
+
+    def halo_odd(i):
+        for k in range(2):
+            arrived(kv.at[2 * i + 1, k], ky_s.at[i, k], kv_r.at[2 * i + 1, k], to_y)
+            sends.append(ky_copy(i, k))
+
+    w_hop(2, late)
+    halo(0)
+    u_take(1)
+    w_hop(3, late)
+    halo(1)
+    project(1, 0, 7)
+    for n in late:
+        w_wait(4, n)
+    project(1, 7, 8)
+    project_out(1)
+    halo(2)
+    for p in range(2):
+        arrived(u_rows(p, from_c), x_s.at[4 + p], x_r.at[4 + p], to_c)
+    project(2, 0, 8)
+    project_out(2)
+    halo(3)
+
+    for h in range(2):
+        mb[h] = jnp.full((B, HD), -3e38, F32)
+        lb[h] = jnp.zeros((B, HD), F32)
+        oacc[h] = jnp.zeros((B, HD), F32)
+        dqa[h] = jnp.zeros((B, HD), F32)
     both = total(1)
     for h in range(2):
         q = rot(both[:, h * HD : (h + 1) * HD], 1.0)
@@ -254,69 +313,37 @@
         dob[h] = v.astype(BF)
         dot_[h] = jnp.transpose(v).astype(BF)
 
-    mb[...] = jnp.full(mb.shape, -3e38, F32)
     diff = lax.broadcasted_iota(jnp.int32, (B, B), 1) - lax.broadcasted_iota(jnp.int32, (B, B), 0)
 
-    def scores(d, _):
+    def attend(d, _):
         top = jnp.where(s >= d, d * B, -2 * WINDOW)
         allowed = (diff <= top) & (diff > d * B - WINDOW)
         for h in range(2):
             sc = jnp.where(allowed, nt(qb[h], kv[d, 0]) * SCALE, -1e30)
-            sb[h, d] = sc
-            mb[h] = jnp.maximum(mb[h], jnp.maximum(sc[:, :HD], sc[:, HD:]))
             db[h, d] = nt(dob[h], kv[d, 1])
+            before = mb[h]
+            peak = jnp.max(jnp.maximum(sc[:, :HD], sc[:, HD:]), axis=1, keepdims=True)
+            now = jnp.maximum(before, peak)
+            e = jnp.exp(sc - jnp.concatenate([now, now], axis=1))
+            keep = jnp.exp(before - now)
+            sb[h, d] = e
+            mb[h] = now
+            msl[h, d] = now
+            lb[h] = lb[h] * keep + e[:, :HD] + e[:, HD:]
+            oacc[h] = oacc[h] * keep + nn(e.astype(BF), kv[d, 1])
         return 0
 
-    for i in range(4):
-        for k in range(2):
-            arrived(kv.at[2 * i + 2, k], kz_s.at[i, k], kv_r.at[2 * i + 2, k], {"z": zr_})
-            if i < 3:
-                kz_send(i + 1, k)
-
-                @pl.when(y == 0)
-                def _():
-                    ky_copy(i + 1, k).start()
-
-            @pl.when(y == 1)
-            def _():
-                ky_copy(i, k).start()
-
-    for i in range(4):
-        for k in range(2):
-            arrived(kv.at[2 * i + 1, k], ky_s.at[i, k], kv_r.at[2 * i + 1, k], to_y)
-            sends.append(ky_copy(i, k))
-    lax.fori_loop(0, 9, scores, 0)
+    lax.fori_loop(0, 1, attend, 0)
+    for i in range(3):
+        halo_odd(i)
+    lax.fori_loop(1, 7, attend, 0)
+    halo_odd(3)
+    lax.fori_loop(7, 9, attend, 0)
 
     for h in range(2):
-        m = jnp.broadcast_to(jnp.max(mb[h], axis=1, keepdims=True), (B, HD))
-        mb[h] = m
-        lb[h] = jnp.zeros((B, HD), F32)
-
-    def exps(d, _):
-        for h in range(2):
-            m = mb[h]
-            e = jnp.exp(sb[h, d] - jnp.concatenate([m, m], axis=1))
-            sb[h, d] = e
-            lb[h] += e[:, :HD] + e[:, HD:]
-        return 0
-
-    lax.fori_loop(0, 9, exps, 0)
-    for h in range(2):
-        lb[h] = jnp.broadcast_to(1.0 / jnp.sum(lb[h], axis=1, keepdims=True), (B, HD))
-        oacc[h] = jnp.zeros((B, HD), F32)
-        dqa[h] = jnp.zeros((B, HD), F32)
-
-    def attend(d, _):
-        for h in range(2):
-            l = lb[h]
-            p = sb[h, d] * jnp.concatenate([l, l], axis=1)
-            sb[h, d] = p
-            oacc[h] += nn(p.astype(BF), kv[d, 1])
-        return 0
-
-    lax.fori_loop(0, 9, attend, 0)
-    for h in range(2):
-        att = oacc[h].astype(BF)
+        scale = jnp.broadcast_to(1.0 / jnp.sum(lb[h], axis=1, keepdims=True), (B, HD))
+        lb[h] = scale
+        att = (oacc[h] * scale).astype(BF)
         dl[2, own, pl.ds(h * HD, HD)] = att
         delta[h] = jnp.broadcast_to(
             jnp.sum(att.astype(F32) * dob[h].astype(F32), axis=1, keepdims=True), (B, HD)
@@ -331,7 +358,8 @@
         dkt = jnp.zeros((HD, B), F32)
         dvt = jnp.zeros((HD, B), F32)
         for h in range(2):
-            p = sb[h, d]
+            f = jnp.exp(msl[h, d] - mb[h]) * lb[h]
+            p = sb[h, d] * jnp.concatenate([f, f], axis=1)
             r = delta[h]
             ds = (p * (db[h, d] - jnp.concatenate([r, r], axis=1)) * SCALE).astype(BF)
             dqa[h] += nn(ds, kv[d, 0])
@@ -339,33 +367,36 @@
             dvt = dvt + nn(dot_[h], p.astype(BF))
         return dkt, dvt
 
-    def y_copy(i):
-        return rc(ysrc.at[i], yrcv.at[i], yr_s.at[i], yr_r.at[i], to_y)
+    def y_copy(i, k):
+        return rc(ysrc.at[i, k], yrcv.at[i, k], yr_s.at[i, k], yr_r.at[i, k], to_y)
 
     def slot_pair(i):
-        a, b = slot_grads(2 * i + 1)
-        ysrc[i, 0] = a.astype(BF)
-        ysrc[i, 1] = b.astype(BF)
-        y_copy(i).start()
-        sends.append(y_copy(i))
-        a, b = slot_grads(2 * i + 2)
-        dkve[i + 1, 0] = a
-        dkve[i + 1, 1] = b
-
-    def from_partner(e):
+        for k, part in enumerate(slot_grads(2 * i + 1)):
+            ysrc[i, k] = part.astype(BF)
+            y_copy(i, k).start()
+            sends.append(y_copy(i, k))
+        for k, part in enumerate(slot_grads(2 * i + 2)):
+            dkve[i + 1, k] = part
+
+    def from_partner(e, k):
         i = e // 2 - y
         keep = jnp.where((i >= 0) & (i < 4), 1.0, 0.0)
-        return yrcv[jnp.clip(i, 0, 3)].astype(F32) * keep
+        return yrcv[jnp.clip(i, 0, 3), k].astype(F32) * keep
+
+    def chain_sum(i, k):
+        e = 8 - 2 * i
+        if i < 4:
+            y_copy(3 - i, k).wait_recv()
+        part = dkve[e // 2, k] + from_partner(e, k)
+        if i > 0:
+            arrived(zrcv.at[i - 1, k], zr_s.at[i - 1, k], zr_r.at[i - 1, k], {"z": zl_})
+            part = part + zrcv[i - 1, k].astype(F32)
+        return part
 
     def chain(i):
-        e = 8 - 2 * i
-        y_copy(3 - i).wait_recv()
-        part = dkve[e // 2] + from_partner(e)
-        if i > 0:
-            arrived(zrcv.at[i - 1], zr_s.at[i - 1], zr_r.at[i - 1], {"z": zl_})
-            part = part + zrcv[i - 1].astype(F32)
-        zsrc[i] = part.astype(BF)
-        send(zsrc.at[i], zrcv.at[i], zr_s.at[i], zr_r.at[i], {"z": zl_})
+        for k in range(2):
+            zsrc[i, k] = chain_sum(i, k).astype(BF)
+            send(zsrc.at[i, k], zrcv.at[i, k], zr_s.at[i, k], zr_r.at[i, k], {"z": zl_})
 
     def dlt_make(ch):
         dlt[ch] = jnp.transpose(dl[ch].astype(F32)).astype(BF)
@@ -388,38 +419,33 @@
         copy.start()
         sends.append(copy)
 
-    slot_pair(3)
-    slot_pair(2)
-    chain(0)
-    slot_pair(1)
-    chain(1)
-    slot_pair(0)
-    a, b = slot_grads(0)
-    dkve[0, 0] = a
-    dkve[0, 1] = b
+    def query_parts(b, _):
+        npart[b] = nt(dl[1], wbuf[b, 1])
+        return 0
+
+    for i in (3, 2, 1, 0):
+        slot_pair(i)
+    for k, part in enumerate(slot_grads(0)):
+        dkve[0, k] = part
     for h in range(2):
         dl[1, own, pl.ds(h * HD, HD)] = rot(dqa[h], -1.0).astype(BF)
+    chain(0)
     dl_send(1)
-    chain(2)
     arrived(dl.at[2, oth, :], d_s.at[2], d_r.at[2], to_y)
     dlt_make(2)
     g(0, 0, 2)
-    chain(3)
+    chain(1)
     arrived(dl.at[1, oth, :], d_s.at[1], d_r.at[1], to_y)
     dlt_make(1)
     g(0, 0, 1)
+    chain(2)
+    lax.fori_loop(0, NZ, query_parts, 0)
+    chain(3)
     g(0, 1, 2)
-
-    def query_parts(b, _):
-        npart[b] = nt(dl[1], wbuf[b, 1])
-        return 0
-
-    lax.fori_loop(0, NZ, query_parts, 0)
-
-    arrived(zrcv.at[3], zr_s.at[3], zr_r.at[3], {"z": zl_})
-    part = dkve[0] + from_partner(0) + zrcv[3].astype(F32)
-    dk = jnp.transpose(part[0])
-    dv = jnp.transpose(part[1])
+    g(0, 1, 1)
+
+    dk = jnp.transpose(chain_sum(4, 0))
+    dv = jnp.transpose(chain_sum(4, 1))
     dl[0, own, pl.ds(0, HD)] = rot(dk, -1.0).astype(BF)
     dl[0, own, pl.ds(HD, HD)] = dv.astype(BF)
     dl_send(0)
@@ -474,7 +500,6 @@
         arrived(rsr.at[way, k], n_s.at[way, k], n_r.at[way, k], {"x": xp})
 
     parts(0, own)
-    g(0, 1, 1)
     pair_sum(0, own)
     r_send(0, 0, xa, own)
     r_send(1, 0, xm, own)
@@ -628,7 +653,8 @@
     for copy in sends:
         copy.wait_send()
     x_out.wait_send()
-    u_out.wait_send()
+    for copy in u_out:
+        copy.wait_send()
 
 
 def finish(og, gq, gk, gv, go, gg, passed, oq, ok, ov, oo, gain_sum):
@@ -661,7 +687,7 @@
         vm((2 * B, HD), F32), vm((8, B), F32), vm((8, B), F32), vm((3, 2 * B, B), F32),
         vm((3, B, B), BF), vm((3, B, B), BF), vm((B, HD), F32), vm((B, HD), F32),
         vm((2, B, HD), BF), vm((9, 2, B, HD), BF), vm((2, B, HD), BF), vm((2, HD, B), BF), vm((2, HD, B), BF),
-        vm((2, 9, B, B), F32), vm((2, 9, B, B), F32),
+        vm((2, 9, B, B), F32), vm((2, 9, B, B), F32), vm((2, 9, B, HD), F32),
         vm((2, B, HD), F32), vm((2, B, HD), F32), vm((2, B, HD), F32), vm((2, B, HD), F32), vm((2, B, HD), F32),
         vm((5, 2, HD, B), F32), vm((4, 2, HD, B), BF), vm((4, 2, HD, B), BF), vm((4, 2, HD, B), BF), vm((4, 2, HD, B), BF),
         vm((3, 2 * B, B), BF), vm((3, B, 2 * B), BF),
@@ -671,8 +697,8 @@
         vm((2, 3, B, B), BF), vm((2, 3, B, B), BF), vm((2 * B, B), F32), vm((2 * B, B), BF),
         vm((NZ, 8, B), F32),
         dma((4,)), dma, dma, dma,
-        dma((2, 4, 3)), dma((2, 4, 3)), dma((4,)), dma((4,)), dma, dma, dma((3,)), dma((3,)),
-        dma((4, 2)), dma((4, 2)), dma((9, 2)), dma((4,)), dma((4,)), dma((4,)), dma((4,)), dma((3,)), dma((3,)),
+        dma((2, 4, 6)), dma((2, 4, 6)), dma((6,)), dma((6,)), dma, dma, dma((3,)), dma((3,)),
+        dma((4, 2)), dma((4, 2)), dma((9, 2)), dma((4, 2)), dma((4, 2)), dma((4, 2)), dma((4, 2)), dma((3,)), dma((3,)),
         dma((5,)), dma((5,)), dma((2, 4, 3)), dma((2, 4, 3)), dma((2, 4)), dma((2, 4)), dma((2, 3)), dma((2, 3)),
         dma((3,)), dma((3,)),
         dma((14,)), dma((14,)), dma((2, 4)), dma((2, 4)), dma, dma,

time: 146 us -> 134 us (0.918)
  Pallas kernels: 146 us -> 133 us
    pallas_call x1, Pallas kernels: 142 us -> 129 us  [per_device(): pl.pallas_call(kernel, out_shape=[jax.ShapeDtypeStruct((8, 2, B, B), BF),...]
where the time goes in v3:
time: 134 us; the launch traced here: 133 us
  Pallas kernels  133 us (99%)
    pallas_call x1, Pallas kernels, per_device(): pl.pallas_call(kernel, out_shape=[jax.ShapeDtypeStruct((8, 2, B, B), BF),...  129 us
    pallas_call x1, Pallas kernels, per_device(): pl.pallas_call(finish, out_shape=[jax.ShapeDtypeStruct((1, B, D), BF), ja...  3.36 us

profile of v3, /device:TPU:1, one launch (start us, length us, event | category | flops | bytes accessed | tf_op | source)
XLA Modules:
  0.0 133.5 jit_solution(2724604528205452448)
XLA Ops:
  0.6 129.5 %step.1 = (bf16[8,2,256,256]{3,2,1,0:T(8,128)(2,1)}, bf16[256,256]{1,0:T(8,128)(2,1)}, bf16[256,128]{1,0:T(8,128)(2,1)}, bf16[256,128]{1,0:T(8,128)(2,1)}, bf16[...) custom-call(bf16[256,4096]{1,0:T(8,128)(2,1)} %bitcast.6, bf16[256,4096]{1,0:T(8,128)(2,1)} %bitcast.7, ...), custom_call_target="tpu_custom_call" | custom-call | tf_op jit(solution)/shard_map/step/pallas_call | solution.py:708
  130.1 3.4 %finish.1 = (bf16[1,256,4096]{2,1,0:T(8,128)(2,1)}, bf16[1,256,256]{2,1,0:T(8,128)(2,1)}, bf16[1,256,128]{2,1,0:T(8,128)(2,1)}, bf16[1,256,128]{2,1,0:T(8,128)(2...) custom-call(bf16[8,2,256,256]{3,2,1,0:T(8,128)(2,1)} %get-tuple-element.12.og, ...), custom_call_target="tpu_custom_call" | custom-call | tf_op jit(solution)/shard_map/finish/pallas_call | solution.py:729

commit v4 on v3

v4 whole, which is shorter than its diff:
```python
import math

import jax
import jax.numpy as jnp
import numpy as np
from jax import lax
from jax.experimental import pallas as pl
from jax.experimental.pallas import tpu as pltpu
from jax.sharding import Mesh
from jax.sharding import PartitionSpec as P

AXES = ("section", "z", "y", "x", "c")
MESH = pl.DeviceIdType.MESH
D = 4096
HD = 128
WINDOW = 2048
B = 256
NZ = 8
NX = 4
EPS = 1e-05
SCALE = 1.0 / math.sqrt(HD)
F32 = jnp.float32
BF = jnp.bfloat16
RIGHT = (4, 3, 4, 3, 3, 3)
LEFT = (3, 4, 3, 4, 4, 4)


def nt(a, b):
    return lax.dot_general(a, b, (((1,), (1,)), ((), ())), preferred_element_type=F32)


def nn(a, b):
    return lax.dot_general(a, b, (((1,), (0,)), ((), ())), preferred_element_type=F32)


def kernel(
    x_hbm, u_hbm, qw, kw, vw, ow, gain_hbm, off_hbm, blk_hbm,
    og, gq, gk, gv, go, gg,
    gain, off, turn, gainf, rel, wbuf, xs, xr, xin, invb, isend, irecv, acc, pbuf, rbuf, cosb, sinb,
    qb, kv, dob, qt, dot_, sb, msl, mb, lb, oacc, dqa, delta,
    dkve, ysrc, yrcv, zsrc, zrcv, dl, dlt, rds, rdr, rdx, rdy, rdb,
    gs, gr, npart, cs, cr, rss, rsr, nd, ps, gb,
    l_w, l_x, l_u, l_r,
    w_s, w_r, x_s, x_r, i_s, i_r, p_s, p_r,
    kz_s, ky_s, kv_r, yr_s, yr_r, zr_s, zr_r, d_s, d_r,
    rd_s, rd_r, g_s, g_r, c_s, c_r, n_s, n_r, ps_s, ps_r,
    og_s, og_r, gb_s, gb_r, gy_s, gy_r,
):
    sec = lax.axis_index("section")
    z = lax.axis_index("z")
    y = lax.axis_index("y")
    x = lax.axis_index("x")
    c = lax.axis_index("c")
    s = 2 * z + y
    t = 2 * x + c
    zr_, zl_ = lax.rem(z + 1, NZ), lax.rem(z + NZ - 1, NZ)
    xp, xm, xa = lax.rem(x + 1, NX), lax.rem(x + NX - 1, NX), lax.rem(x + 2, NX)
    py, pc, psec = 1 - y, 1 - c, 1 - sec
    to_y = {"y": py}
    to_c = {"c": pc}
    own = pl.ds(pl.multiple_of(y * B, B), B)
    oth = pl.ds(pl.multiple_of(py * B, B), B)

    def rc(src, dst, ss, rs, dev):
        return pltpu.make_async_remote_copy(
            src_ref=src, dst_ref=dst, send_sem=ss, recv_sem=rs,
            device_id=dev, device_id_type=MESH,
        )

    sends = []
    marks = [0, 0]

    def drain():
        for copy in sends[marks[0] : marks[1]]:
            copy.wait_send()
        marks[:] = [marks[1], len(sends)]

    def send(src, dst, ss, rs, dev):
        copy = rc(src, dst, ss, rs, dev)
        copy.start()
        sends.append(copy)
        return copy

    def arrived(dst, ss, rs, dev):
        rc(dst, dst, ss, rs, dev).wait_recv()

    loads = [
        pltpu.make_async_copy(kw, wbuf.at[z, 0, :, pl.ds(0, HD)], l_w.at[0]),
        pltpu.make_async_copy(vw, wbuf.at[z, 0, :, pl.ds(HD, HD)], l_w.at[1]),
        pltpu.make_async_copy(qw, wbuf.at[z, 1], l_w.at[2]),
        pltpu.make_async_copy(ow, wbuf.at[z, 2], l_w.at[3]),
        pltpu.make_async_copy(x_hbm, xin, l_x),
        pltpu.make_async_copy(gain_hbm, gain, l_w.at[4]),
        pltpu.make_async_copy(off_hbm, off, l_w.at[5]),
        pltpu.make_async_copy(blk_hbm, turn, l_w.at[6]),
    ]
    for copy in loads:
        copy.start()

    def cols(blk, parity):
        return pl.ds(pl.multiple_of((2 * blk + parity) * B, B), B)

    for j in range(NZ):
        pltpu.make_async_copy(u_hbm.at[:, cols(j, y)], xs.at[1, j, own, :], l_u).start()
        pltpu.make_async_copy(x_hbm.at[:, cols(j, y)], xr.at[j, own, :], l_r).start()

    barrier = pltpu.get_barrier_semaphore()
    greet = [
        {"z": zr_}, {"z": zl_}, to_y, to_c, {"x": xp}, {"x": xm}, {"x": xa},
        {"section": psec, "y": py},
    ]
    for dev in greet:
        pl.semaphore_signal(barrier, inc=1, device_id=dev, device_id_type=MESH)
    pl.semaphore_wait(barrier, len(greet))

    for copy in loads[:4]:
        copy.wait()

    def w_half(blk, n):
        return wbuf.at[blk, n // 2, :, pl.ds(n % 2 * HD, HD)]

    def w_copy(way, h, n):
        blk = lax.rem(z + NZ - h, NZ) if way == 0 else lax.rem(z + h, NZ)
        dev = {"z": zr_ if way == 0 else zl_}
        return rc(w_half(blk, n), w_half(blk, n), w_s.at[way, h, n], w_r.at[way, h, n], dev)

    def w_send(h, n):
        for way, hops in ((0, RIGHT), (1, LEFT)):
            if h < hops[n]:
                copy = w_copy(way, h, n)
                copy.start()
                sends.append(copy)

    def w_wait(h, n):
        for way, hops in ((0, RIGHT), (1, LEFT)):
            if h <= hops[n]:
                blk = lax.rem(z + NZ - h, NZ) if way == 0 else lax.rem(z + h, NZ)
                arrived(w_half(blk, n), w_s.at[way, h - 1, n], w_r.at[way, h - 1, n], {"z": zr_})

    def w_hop(h, halves):
        for n in halves:
            w_wait(h, n)
            w_send(h, n)

    early, late = (0, 1, 2), (3, 4, 5)
    for n in early:
        w_send(0, n)

    mine = pl.ds(pl.multiple_of(c * 128, 128), 128)
    there = pl.ds(pl.multiple_of(y * B + c * 128, 128), 128)
    from_y = pl.ds(pl.multiple_of(py * B + c * 128, 128), 128)
    from_c = pl.ds(pl.multiple_of(py * B + pc * 128, 128), 128)
    for j in range(NZ):
        rc(x_hbm.at[mine, cols(j, py)], xr.at[j, there, :], x_s.at[0], x_r.at[0], to_y).start()
    x_out = rc(xr.at[:, from_y, :], xr.at[:, there, :], x_s.at[0], x_r.at[0], to_y)

    for copy in loads[5:]:
        copy.wait()
    for j in range(D // B):
        gainf[j] = gain[:, j * B : (j + 1) * B].astype(F32)

    lane = lax.broadcasted_iota(jnp.int32, (B, HD), 1)
    cosb[...] = turn[0, s] * off[0] - turn[1, s] * off[1]
    sin_all = turn[1, s] * off[0] + turn[0, s] * off[1]
    sinb[...] = jnp.where(lane < HD // 2, -sin_all, sin_all)

    loads[4].wait()
    invb[own, :] = jnp.zeros((B, HD), F32)

    def squares(j, _):
        v = xin[:, pl.ds(pl.multiple_of(j * B, B), B)].astype(F32)
        invb[own, :] += v[:, :HD] * v[:, :HD] + v[:, HD:] * v[:, HD:]
        return 0

    lax.fori_loop(0, D // B, squares, 0)
    mean = jnp.sum(invb[own, :], axis=1, keepdims=True) / D
    inv_own = jnp.broadcast_to(lax.rsqrt(mean + EPS), (B, HD))
    invb[own, :] = inv_own
    isend[...] = jnp.transpose(inv_own)[:8, :]
    send(isend, irecv, i_s, i_r, to_y)

    odd = lax.rem(x, 2)
    to_n = {"x": x + 1 - 2 * odd}

    def u_rows(side, px, core):
        return xs.at[1, :, pl.ds(pl.multiple_of(side * B + px * 128 + core * 64, 64), 64), :]

    quarter = pl.ds(pl.multiple_of(odd * 128 + c * 64, 64), 64)
    row0 = pl.ds(pl.multiple_of(y * B + odd * 128 + c * 64, 64), 64)
    for j in range(NZ):
        rc(u_hbm.at[quarter, cols(j, py)], xs.at[1, j, row0, :], x_s.at[1], x_r.at[1], to_y).start()
    u_out = rc(u_rows(py, odd, c), u_rows(y, odd, c), x_s.at[1], x_r.at[1], to_y)

    def u_take(part):
        if part == 0:
            u_out.wait_recv()
            send(u_rows(py, odd, c), u_rows(py, odd, c), x_s.at[3], x_r.at[3], to_n)
            send(u_rows(py, odd, c), u_rows(py, odd, c), x_s.at[4], x_r.at[4], to_c)
        else:
            arrived(u_rows(py, 1 - odd, c), x_s.at[3], x_r.at[3], to_n)
            send(u_rows(py, 1 - odd, c), u_rows(py, 1 - odd, c), x_s.at[5], x_r.at[5], to_c)

    def u_rest():
        arrived(u_rows(py, odd, pc), x_s.at[4], x_r.at[4], to_c)
        arrived(u_rows(py, 1 - odd, pc), x_s.at[5], x_r.at[5], to_c)

    whole = pltpu.make_async_copy(xs.at[1, :, oth, :], xs.at[1, :, own, :], l_u)
    whole.wait()
    pltpu.make_async_copy(xr.at[:, oth, :], xr.at[:, own, :], l_r).wait()

    def norm_rows(rows):
        def step(j, _):
            inv = invb[rows, :]
            g = gainf[2 * j + y]
            v = xr[j, rows, :].astype(F32)
            n = jnp.concatenate([v[:, :HD] * inv, v[:, HD:] * inv], axis=1) * g
            xs[0, j, rows, :] = n.astype(BF)
            return 0

        lax.fori_loop(0, NZ, step, 0)

    norm_rows(own)

    w_hop(1, early)
    w_hop(2, early)
    x_out.wait_recv()
    send(xr.at[:, from_y, :], xr.at[:, from_y, :], x_s.at[2], x_r.at[2], to_c)
    w_hop(3, (0,))
    arrived(irecv, i_s, i_r, to_y)
    inv_oth = jnp.transpose(jnp.broadcast_to(irecv[0:1, :], (HD, B)))
    invb[oth, :] = inv_oth
    arrived(xr.at[:, from_c, :], x_s.at[2], x_r.at[2], to_c)
    norm_rows(oth)
    w_hop(3, (1,))

    def project(ch, lo, hi, start=0, width=B):
        at = pl.ds(start, width)

        def step(n, _):
            blk = lax.rem(z + 5 + n, NZ)
            acc[ch, :, at] += nn(xs[1 if ch == 2 else 0, blk], wbuf[blk, ch, :, at])
            return 0

        lax.fori_loop(lo, hi, step, 0)

    def p_copy(n):
        ch = (0, 1, 1, 2, 2)[n]
        at = (pl.ds(0, B), pl.ds(0, HD), pl.ds(HD, HD), pl.ds(0, HD), pl.ds(HD, HD))[n]
        return rc(pbuf.at[ch, :, at], rbuf.at[ch, :, at], p_s.at[n], p_r.at[n], to_y)

    def project_out(n):
        ch = (0, 1, 1, 2, 2)[n]
        at = (pl.ds(0, B), pl.ds(0, HD), pl.ds(HD, HD), pl.ds(0, HD), pl.ds(HD, HD))[n]
        pbuf[ch, :, at] = acc[ch, oth, at].astype(BF)
        p_copy(n).start()
        sends.append(p_copy(n))

    def total(n):
        p_copy(n).wait_recv()
        ch = (0, 1, 1, 2, 2)[n]
        at = (pl.ds(0, B), pl.ds(0, HD), pl.ds(HD, HD), pl.ds(0, HD), pl.ds(HD, HD))[n]
        return acc[ch, own, at] + rbuf[ch, :, at].astype(F32)

    def rot(v, sign):
        return v * cosb[...] + pltpu.roll(v, HD // 2, 1) * (sign * sinb[...])

    acc[...] = jnp.zeros_like(acc)
    project(0, 1, 6)
    w_hop(3, (2,))
    for n in late:
        w_send(0, n)
    project(0, 0, 1)
    project(0, 6, 7)
    for n in early:
        w_wait(4, n)
    project(0, 7, 8)
    project_out(0)
    project(1, 0, 8, 0, HD)
    project_out(1)
    w_hop(1, late)
    u_take(0)
    both = total(0)
    kv[0, 0] = rot(both[:, :HD], 1.0).astype(BF)
    kv[0, 1] = both[:, HD:].astype(BF)

    def kz_send(i, k):
        send(kv.at[2 * i, k], kv.at[2 * i + 2, k], kz_s.at[i, k], kv_r.at[2 * i + 2, k], {"z": zr_})

    def ky_copy(i, k):
        return rc(kv.at[2 * i + 2 * y, k], kv.at[2 * i + 1, k], ky_s.at[i, k], kv_r.at[2 * i + 1, k], to_y)

    def ky_start(i, k, side):
        @pl.when(y == side)
        def _():
            ky_copy(i, k).start()

    for k in range(2):
        kz_send(0, k)
        ky_start(0, k, 0)

    def halo(i):
        for k in range(2):
            arrived(kv.at[2 * i + 2, k], kz_s.at[i, k], kv_r.at[2 * i + 2, k], {"z": zr_})
            if i < 3:
                kz_send(i + 1, k)
                ky_start(i + 1, k, 0)
            ky_start(i, k, 1)

    def halo_odd(i):
        for k in range(2):
            arrived(kv.at[2 * i + 1, k], ky_s.at[i, k], kv_r.at[2 * i + 1, k], to_y)
            sends.append(ky_copy(i, k))

    drain()
    w_hop(2, (3,))
    halo(0)
    w_hop(2, (4, 5))
    w_hop(3, (3,))
    halo(1)
    drain()
    w_hop(3, (4, 5))
    u_take(1)
    project(1, 0, 7, HD, HD)
    u_rest()
    halo(2)
    w_wait(4, 3)
    project(1, 7, 8, HD, HD)
    project_out(2)
    project(2, 0, 7)
    w_wait(4, 4)
    project(2, 7, 8, 0, HD)
    project_out(3)
    w_wait(4, 5)
    project(2, 7, 8, HD, HD)
    project_out(4)
    drain()
    halo(3)

    for h in range(2):
        mb[h] = jnp.full((B, HD), -3e38, F32)
        lb[h] = jnp.zeros((B, HD), F32)
        oacc[h] = jnp.zeros((B, HD), F32)
        dqa[h] = jnp.zeros((B, HD), F32)
    for h in range(2):
        q = rot(total(1 + h), 1.0)
        qb[h] = q.astype(BF)
        qt[h] = jnp.transpose(q).astype(BF)

    diff = lax.broadcasted_iota(jnp.int32, (B, B), 1) - lax.broadcasted_iota(jnp.int32, (B, B), 0)

    def attend(group):
        slots = [3 * group + j for j in range(3)]
        for h in range(2):
            before = mb[h]
            scores = []
            peak = None
            for d in slots:
                top = jnp.where(s >= d, d * B, -2 * WINDOW)
                allowed = (diff <= top) & (diff > d * B - WINDOW)
                sc = jnp.where(allowed, nt(qb[h], kv[d, 0]) * SCALE, -1e30)
                sb[h, d] = sc
                both = jnp.maximum(sc[:, :HD], sc[:, HD:])
                peak = both if peak is None else jnp.maximum(peak, both)
            now = jnp.maximum(before, jnp.max(peak, axis=1, keepdims=True))
            keep = jnp.exp(before - now)
            mb[h] = now
            msl[h, group] = now
            total_l = lb[h] * keep
            total_o = oacc[h] * keep
            for d in slots:
                e = jnp.exp(sb[h, d] - jnp.concatenate([now, now], axis=1))
                sb[h, d] = e
                total_l = total_l + e[:, :HD] + e[:, HD:]
                total_o = total_o + nn(e.astype(BF), kv[d, 1])
            lb[h] = total_l
            oacc[h] = total_o

    halo_odd(0)
    attend(0)
    halo_odd(1)
    halo_odd(2)
    attend(1)
    halo_odd(3)
    attend(2)
    for h in range(2):
        v = total(3 + h)
        dob[h] = v.astype(BF)
        dot_[h] = jnp.transpose(v).astype(BF)

    for h in range(2):
        scale = jnp.broadcast_to(1.0 / jnp.sum(lb[h], axis=1, keepdims=True), (B, HD))
        lb[h] = scale
        att = (oacc[h] * scale).astype(BF)
        dl[2, own, pl.ds(h * HD, HD)] = att
        delta[h] = jnp.broadcast_to(
            jnp.sum(att.astype(F32) * dob[h].astype(F32), axis=1, keepdims=True), (B, HD)
        )

    def dl_send(ch):
        send(dl.at[ch, own, :], dl.at[ch, own, :], d_s.at[ch], d_r.at[ch], to_y)

    def slot_grads(d):
        dkt = jnp.zeros((HD, B), F32)
        dvt = jnp.zeros((HD, B), F32)
        for h in range(2):
            f = jnp.exp(msl[h, d // 3] - mb[h]) * lb[h]
            p = sb[h, d] * jnp.concatenate([f, f], axis=1)
            r = delta[h]
            ds = (p * (nt(dob[h], kv[d, 1]) - jnp.concatenate([r, r], axis=1)) * SCALE).astype(BF)
            dqa[h] += nn(ds, kv[d, 0])
            dkt = dkt + nn(qt[h], ds)
            dvt = dvt + nn(dot_[h], p.astype(BF))
        return dkt, dvt

    def piece(ref, p):
        return ref.at[p // 2, pl.ds(p % 2 * 64, 64), :]

    def y_copy(i, p):
        return rc(piece(ysrc.at[i], p), piece(yrcv.at[i], p), yr_s.at[i, p], yr_r.at[i, p], to_y)

    def slot_pair(i):
        for k, part in enumerate(slot_grads(2 * i + 1)):
            ysrc[i, k] = part.astype(BF)
        for p in range(4):
            y_copy(i, p).start()
            sends.append(y_copy(i, p))
        for k, part in enumerate(slot_grads(2 * i + 2)):
            dkve[i + 1, k] = part

    def from_partner(e, p):
        i = e // 2 - y
        keep = jnp.where((i >= 0) & (i < 4), 1.0, 0.0)
        return yrcv[jnp.clip(i, 0, 3), p // 2, pl.ds(p % 2 * 64, 64), :].astype(F32) * keep

    def chain_sum(i, p):
        e = 8 - 2 * i
        if i < 4:
            y_copy(3 - i, p).wait_recv()
        rows = pl.ds(p % 2 * 64, 64)
        part = dkve[e // 2, p // 2, rows, :] + from_partner(e, p)
        if i > 0:
            arrived(piece(zrcv.at[i - 1], p), zr_s.at[i - 1, p], zr_r.at[i - 1, p], {"z": zl_})
            part = part + zrcv[i - 1, p // 2, rows, :].astype(F32)
        return part

    def chain(i):
        for p in range(4):
            zsrc[i, p // 2, pl.ds(p % 2 * 64, 64), :] = chain_sum(i, p).astype(BF)
            send(piece(zsrc.at[i], p), piece(zrcv.at[i], p), zr_s.at[i, p], zr_r.at[i, p], {"z": zl_})

    def dlt_make(ch):
        dlt[ch] = jnp.transpose(dl[ch].astype(F32)).astype(BF)

    hops = ((3, 4, 4), (4, 3, 3))

    def g_copy(way, j, ch):
        dev = {"z": zr_ if way == 0 else zl_}
        return rc(gs.at[way, j, ch], gr.at[way, j, ch], g_s.at[way, j, ch], g_r.at[way, j, ch], dev)

    def weight_part(blk, ch):
        return nn(dlt[ch], xs[1 if ch == 2 else 0, blk])

    def g(way, j, ch):
        left = hops[way][ch] - j
        step = left if way == 0 else NZ - left
        part = weight_part(lax.rem(z + step, NZ), ch)
        if j > 0:
            g_copy(way, j - 1, ch).wait_recv()
            part = part + gr[way, j - 1, ch].astype(F32)
        gs[way, j, ch] = part.astype(BF)
        copy = g_copy(way, j, ch)
        copy.start()
        sends.append(copy)

    def query_parts(rows):
        def step(b, _):
            npart[b, rows, :] = nt(dl[1, rows, :], wbuf[b, 1])
            return 0

        lax.fori_loop(0, NZ, step, 0)

    slot_pair(3)
    slot_pair(2)
    slot_pair(1)
    slot_pair(0)
    for k, part in enumerate(slot_grads(0)):
        dkve[0, k] = part
    for h in range(2):
        dl[1, own, pl.ds(h * HD, HD)] = rot(dqa[h], -1.0).astype(BF)
    dl_send(2)
    dl_send(1)
    drain()
    chain(0)
    query_parts(own)
    x_out.wait_send()
    u_out.wait_send()
    chain(1)
    chain(2)
    chain(3)
    arrived(dl.at[2, oth, :], d_s.at[2], d_r.at[2], to_y)
    dlt_make(2)
    g(0, 0, 2)

    for p in range(4):
        dkve[0, p // 2, pl.ds(p % 2 * 64, 64), :] = chain_sum(4, p)
    dk = jnp.transpose(dkve[0, 0])
    dv = jnp.transpose(dkve[0, 1])
    dl[0, own, pl.ds(0, HD)] = rot(dk, -1.0).astype(BF)
    dl[0, own, pl.ds(HD, HD)] = dv.astype(BF)
    dl_send(0)

    rd = dk * kv[0, 0].astype(F32) + dv * kv[0, 1].astype(F32)
    for h in range(2):
        rd = rd + dqa[h] * qb[h].astype(F32)
    rd = jnp.broadcast_to(jnp.sum(rd, axis=1, keepdims=True), (B, HD))
    rds[0] = jnp.transpose(rd)[:8, :]
    send(rds.at[0], rdr, rd_s.at[0], rd_r.at[0], to_c)

    def c_copy(k, i, rows):
        return rc(cs.at[i, rows, :], cr.at[i, rows, :], c_s.at[k, i], c_r.at[k, i], to_c)

    def parts(k, rows):
        def out(i, _):
            b = 2 * i + pc
            cs[i, rows, :] = (npart[b, rows, :] + nt(dl[0, rows, :], wbuf[b, 0])).astype(BF)
            c_copy(k, i, rows).start()
            return 0

        def keep(i, _):
            b = 2 * i + c
            npart[b, rows, :] += nt(dl[0, rows, :], wbuf[b, 0])
            return 0

        lax.fori_loop(0, NX, out, 0)
        lax.fori_loop(0, NX, keep, 0)
        for i in range(NX):
            sends.append(c_copy(k, i, rows))

    def pair_sum(k, rows):
        for i in range(NX):
            c_copy(k, i, rows).wait_recv()

        def add(i, _):
            npart[2 * i + c, rows, :] += cr[i, rows, :].astype(F32)
            return 0

        lax.fori_loop(0, NX, add, 0)

    def half_rows(side, q):
        return pl.ds(pl.multiple_of(side * B + q * HD, HD), HD)

    def r_copy(way, k, q):
        dev = {"x": xp} if way == 0 else {"x": xm}
        rows = pl.ds(q * HD, HD)
        return rc(rss.at[way, k, rows, :], rsr.at[way, k, rows, :], n_s.at[way, k, q], n_r.at[way, k, q], dev)

    def r_send(way, k, blk, side, add=None):
        for q in range(2):
            part = npart[2 * blk + c, half_rows(side, q), :]
            if add is not None:
                r_copy(way, add, q).wait_recv()
                part = part + rsr[way, add, pl.ds(q * HD, HD), :].astype(F32)
            rss[way, k, pl.ds(q * HD, HD), :] = part.astype(BF)
            copy = r_copy(way, k, q)
            copy.start()
            sends.append(copy)

    parts(0, own)
    pair_sum(0, own)
    r_send(0, 0, xa, y)
    r_send(1, 0, xm, y)
    arrived(rdr, rd_s.at[0], rd_r.at[0], to_c)
    rds[1] = rds[0] + rdr[...]
    for k, dev in enumerate(({"x": xp}, {"x": xm}, {"x": xa})):
        send(rds.at[1], rdx.at[k], rd_s.at[1 + k], rd_r.at[1 + k], dev)
    arrived(dl.at[1, oth, :], d_s.at[1], d_r.at[1], to_y)
    dlt_make(1)
    g(0, 0, 1)
    g(1, 0, 2)
    g(1, 0, 1)
    g(0, 1, 2)
    drain()

    query_parts(oth)
    arrived(dl.at[0, oth, :], d_s.at[0], d_r.at[0], to_y)
    parts(1, oth)
    pair_sum(1, oth)
    r_send(1, 1, xa, py)
    r_send(0, 1, xp, y, 0)

    dlt_make(0)
    g(1, 0, 0)
    g(0, 0, 0)
    g(0, 1, 1)
    r_send(0, 2, xp, py)
    for k in range(3):
        arrived(rdx.at[k], rd_s.at[1 + k], rd_r.at[1 + k], {"x": xp})
    rds[2] = rds[1] + rdx[0] + rdx[1] + rdx[2]
    send(rds.at[2], rdy, rd_s.at[4], rd_r.at[4], to_y)
    rdb[own, :] = jnp.transpose(jnp.broadcast_to(rds[2, 0:1, :], (HD, B)))
    g(1, 1, 2)
    r_send(1, 2, xm, py, 1)

    def share(side, first, second, target, k):
        for q in range(2):
            rows, at = half_rows(side, q), pl.ds(q * HD, HD)
            r_copy(*first, q).wait_recv()
            r_copy(*second, q).wait_recv()
            n_all = npart[t, rows, :] + rsr[first[0], first[1], at, :].astype(F32)
            n_all = n_all + rsr[second[0], second[1], at, :].astype(F32)
            nd[rows, :] = n_all
            for hf in range(2):
                cut = pl.ds(hf * HD, HD)
                inv = invb[rows, :]
                v = xr[t, rows, cut].astype(F32)
                n = n_all[:, hf * HD : (hf + 1) * HD]
                gn = gainf[2 * t + y, :, cut]
                out = xs[1, t, rows, cut].astype(F32) + inv * gn * n - v * (inv * inv) * rdb[rows, :] * (1.0 / D)
                ps[rows, cut] = out.astype(BF)
            send(ps.at[rows, :], target.at[at, :], ps_s.at[k, q], ps_r.at[k, q], across)

    def gain_term(rows, cut):
        return jnp.sum(nd[rows, cut] * xr[t, rows, cut].astype(F32) * invb[rows, :], axis=0, keepdims=True)

    across = {"section": psec, "y": py}
    share(y, (0, 1), (1, 0), rel, 0)
    g(1, 1, 0)
    g(0, 1, 0)
    g(0, 2, 2)
    g(1, 1, 1)
    arrived(rdy, rd_s.at[4], rd_r.at[4], to_y)
    rdb[oth, :] = jnp.transpose(jnp.broadcast_to(rdy[0:1, :], (HD, B)))
    share(py, (0, 2), (1, 2), og.at[t, y], 1)
    for hf in range(2):
        cut = pl.ds(hf * HD, HD)
        gb[z, :, cut] = jnp.broadcast_to(gain_term(own, cut) + gain_term(oth, cut), (8, HD))

    def gb_send(h):
        blk = lax.rem(z + NZ - h, NZ)
        send(gb.at[blk], gb.at[blk], gb_s.at[0, h], gb_r.at[0, h], {"z": zr_})
        if h < 3:
            blk = lax.rem(z + h, NZ)
            send(gb.at[blk], gb.at[blk], gb_s.at[1, h], gb_r.at[1, h], {"z": zl_})

    def gb_wait(h):
        blk = lax.rem(z + NZ - h, NZ)
        arrived(gb.at[blk], gb_s.at[0, h - 1], gb_r.at[0, h - 1], {"z": zr_})
        if h < 4:
            blk = lax.rem(z + h, NZ)
            arrived(gb.at[blk], gb_s.at[1, h - 1], gb_r.at[1, h - 1], {"z": zl_})

    gb_send(0)
    g(1, 2, 0)
    g(0, 2, 1)
    drain()

    for q in range(2):
        at = pl.ds(q * HD, HD)
        arrived(rel.at[at, :], ps_s.at[0, q], ps_r.at[0, q], across)
        send(rel.at[at, :], og.at[t, py, at, :], ps_s.at[2, q], ps_r.at[2, q], to_y)

    def finish_grad(ch):
        part = weight_part(z, ch)
        for way in range(2):
            last = hops[way][ch] - 1
            g_copy(way, last, ch).wait_recv()
            part = part + gr[way, last, ch].astype(F32)
        part = jnp.transpose(part).astype(BF)
        if ch == 2:
            go[...] = part
        elif ch == 1:
            gq[...] = part
        else:
            gk[...] = part[:, :HD]
            gv[...] = part[:, HD:]

    tr, tl, ta = 2 * xm + c, 2 * xp + c, 2 * xa + c

    def og_half(blk, par, q):
        return og.at[blk, par, pl.ds(q * HD, HD), :]

    def og_send(blk, par, q, k, dev):
        send(og_half(blk, par, q), og_half(blk, par, q), og_s.at[k, q], og_r.at[k, q], dev)

    def og_wait(blk, par, q, k):
        arrived(og_half(blk, par, q), og_s.at[k, q], og_r.at[k, q], to_c)

    g(0, 2, 0)
    for q in range(2):
        arrived(og_half(t, py, q), ps_s.at[1, q], ps_r.at[1, q], across)
        og_send(t, py, q, 0, {"x": xp})
        og_send(t, py, q, 1, {"x": xm})
        og_send(t, py, q, 6, to_c)
    for q in range(2):
        arrived(og_half(t, y, q), ps_s.at[2, q], ps_r.at[2, q], to_y)
        og_send(t, y, q, 2, {"x": xp})
        og_send(t, y, q, 3, {"x": xm})
        og_send(t, y, q, 7, to_c)
    g(1, 3, 0)
    gb_wait(1)
    gb_send(1)
    g(0, 3, 2)
    g(1, 2, 2)
    for q in range(2):
        og_wait(tr, py, q, 0)
        og_send(tr, py, q, 4, {"x": xp})
        og_send(tr, py, q, 8, to_c)
    gb_wait(2)
    gb_send(2)
    g(1, 2, 1)
    g(0, 3, 1)
    for q in range(2):
        og_wait(tl, py, q, 1)
        og_send(tl, py, q, 9, to_c)
    for q in range(2):
        og_wait(tl, y, q, 3)
        og_send(tl, y, q, 5, {"x": xm})
        og_send(tl, y, q, 11, to_c)
    for q in range(2):
        og_wait(tr, y, q, 2)
        og_send(tr, y, q, 10, to_c)
    gb_wait(3)
    gb_send(3)
    drain()
    finish_grad(2)
    finish_grad(1)
    for q in range(2):
        og_wait(ta, py, q, 4)
        og_send(ta, py, q, 12, to_c)
    for q in range(2):
        og_wait(ta, y, q, 5)
        og_send(ta, y, q, 13, to_c)
    gb_wait(4)
    gsum = gb[0]
    for i in range(1, NZ):
        gsum = gsum + gb[i]
    gg[y] = gsum
    send(gg.at[y], gg.at[y], gy_s, gy_r, to_y)
    finish_grad(0)
    drain()

    sib = 1 - 2 * c
    for blk, ks in ((t, (6, 7)), (tr, (8, 10)), (tl, (9, 11)), (ta, (12, 13))):
        for q in range(2):
            og_wait(blk + sib, py, q, ks[0])
            og_wait(blk + sib, y, q, ks[1])
    arrived(gg.at[py], gy_s, gy_r, to_y)
    drain()
    drain()


def finish(og, gq, gk, gv, go, gg, passed, oq, ok, ov, oo, gain_sum, row, sems):
    copies = []
    for blk in range(8):
        for par in range(2):
            at = 2 * blk + par
            copies.append((og.at[blk, par], passed.at[0, :, pl.ds(at * B, B)]))
    copies += [(gq, oq.at[0]), (gk, ok.at[0]), (gv, ov.at[0]), (go, oo.at[0])]
    row[:, :B] = gg[0, 0:1, :]
    row[:, B:] = gg[1, 0:1, :]
    copies.append((row, gain_sum))
    started = [pltpu.make_async_copy(a, b, sems.at[i]) for i, (a, b) in enumerate(copies)]
    for copy in started:
        copy.start()
    for copy in started:
        copy.wait()


def tables():
    freq = 10000.0 ** (-2.0 * np.arange(HD // 2) / HD)
    freq = np.concatenate([freq, freq])
    off = np.arange(B)[:, None] * freq[None, :]
    blk = (np.arange(16) * B)[:, None, None] * freq[None, None, :]
    return [np.stack([np.cos(a), np.sin(a)]).astype(np.float32) for a in (off, blk)]


def per_device(layer_input, upstream, norm_gain, query_weight, key_weight, value_weight, output_weight):
    dma = pltpu.SemaphoreType.DMA
    vm = pltpu.VMEM
    scratch = [
        vm((1, D), BF), vm((2, B, HD), F32), vm((2, 16, 1, HD), F32),
        vm((D // B, 1, B), F32), vm((B, B), BF),
        vm((NZ, 3, B, B), BF), vm((2, NZ, 2 * B, B), BF), vm((NZ, 2 * B, B), BF), vm((B, D), BF),
        vm((2 * B, HD), F32), vm((8, B), F32), vm((8, B), F32), vm((3, 2 * B, B), F32),
        vm((3, B, B), BF), vm((3, B, B), BF), vm((B, HD), F32), vm((B, HD), F32),
        vm((2, B, HD), BF), vm((9, 2, B, HD), BF), vm((2, B, HD), BF), vm((2, HD, B), BF), vm((2, HD, B), BF),
        vm((2, 9, B, B), F32), vm((2, 3, B, HD), F32),
        vm((2, B, HD), F32), vm((2, B, HD), F32), vm((2, B, HD), F32), vm((2, B, HD), F32), vm((2, B, HD), F32),
        vm((5, 2, HD, B), F32), vm((4, 2, HD, B), BF), vm((4, 2, HD, B), BF), vm((4, 2, HD, B), BF), vm((4, 2, HD, B), BF),
        vm((3, 2 * B, B), BF), vm((3, B, 2 * B), BF),
        vm((3, 8, B), F32), vm((8, B), F32), vm((3, 8, B), F32), vm((8, B), F32), vm((2 * B, HD), F32),
        vm((2, 4, 3, B, B), BF), vm((2, 4, 3, B, B), BF),
        vm((NZ, 2 * B, B), F32), vm((NX, 2 * B, B), BF), vm((NX, 2 * B, B), BF),
        vm((2, 3, B, B), BF), vm((2, 3, B, B), BF), vm((2 * B, B), F32), vm((2 * B, B), BF),
        vm((NZ, 8, B), F32),
        dma((7,)), dma, dma, dma,
        dma((2, 4, 6)), dma((2, 4, 6)), dma((6,)), dma((6,)), dma, dma, dma((5,)), dma((5,)),
        dma((4, 2)), dma((4, 2)), dma((9, 2)), dma((4, 4)), dma((4, 4)), dma((4, 4)), dma((4, 4)), dma((3,)), dma((3,)),
        dma((5,)), dma((5,)), dma((2, 4, 3)), dma((2, 4, 3)), dma((2, 4)), dma((2, 4)), dma((2, 3, 2)), dma((2, 3, 2)),
        dma((3, 2)), dma((3, 2)),
        dma((14, 2)), dma((14, 2)), dma((2, 4)), dma((2, 4)), dma, dma,
    ]
    hbm = pl.BlockSpec(memory_space=pl.ANY)
    vmem = pl.BlockSpec(memory_space=pltpu.VMEM)
    og, gq, gk, gv, go, gg = pl.pallas_call(
        kernel,
        out_shape=[
            jax.ShapeDtypeStruct((8, 2, B, B), BF),
            jax.ShapeDtypeStruct((B, B), BF),
            jax.ShapeDtypeStruct((B, HD), BF),
            jax.ShapeDtypeStruct((B, HD), BF),
            jax.ShapeDtypeStruct((B, B), BF),
            jax.ShapeDtypeStruct((2, 8, B), F32),
        ],
        in_specs=[pl.BlockSpec(memory_space=pltpu.HBM)] * 9,
        out_specs=[vmem] * 6,
        scratch_shapes=scratch,
        compiler_params=pltpu.CompilerParams(
            collective_id=0, has_side_effects=True, vmem_limit_bytes=46 * 1024 * 1024
        ),
        name="step",
    )(
        *[pltpu.with_memory_space_constraint(jnp.asarray(a), pltpu.HBM) for a in (layer_input[0], upstream[0], query_weight[0], key_weight[0], value_weight[0], output_weight[0], norm_gain, *tables())],
    )
    return pl.pallas_call(
        finish,
        out_shape=[
            jax.ShapeDtypeStruct((1, B, D), BF),
            jax.ShapeDtypeStruct((1, B, B), BF),
            jax.ShapeDtypeStruct((1, B, HD), BF),
            jax.ShapeDtypeStruct((1, B, HD), BF),
            jax.ShapeDtypeStruct((1, B, B), BF),
            jax.ShapeDtypeStruct((1, 2 * B), F32),
        ],
        in_specs=[vmem] * 6,
        out_specs=[hbm] * 6,
        scratch_shapes=[vm((1, 2 * B), F32), dma((21,))],
        compiler_params=pltpu.CompilerParams(vmem_limit_bytes=8 * 1024 * 1024),
        name="finish",
    )(og, gq, gk, gv, go, gg)


def solution(mesh):
    split = Mesh(mesh.devices.reshape(2, NZ, 2, NX, 2), AXES)
    seq, tp = ("z", "y"), ("x", "c")
    rows = P("section", seq, None)
    weight = P("section", seq, tp)
    return jax.shard_map(
        per_device,
        mesh=split,
        in_specs=(rows, rows, P("section", None), weight, weight, weight, weight),
        out_specs=(rows, weight, weight, weight, weight, P("section", tp)),
        check_vma=False,
    )
```

time: 134 us -> 127 us (0.948)
  Pallas kernels: 133 us -> 126 us
    pallas_call x1, Pallas kernels: 129 us -> 125 us  [per_device(): pl.pallas_call(kernel, out_shape=[jax.ShapeDtypeStruct((8, 2, B, B), BF),...]
    pallas_call x1, Pallas kernels: 3.36 us -> 1.62 us  [per_device(): pl.pallas_call(finish, out_shape=[jax.ShapeDtypeStruct((1, B, D), BF), ja...]
where the time goes in v4:
time: 127 us
  Pallas kernels  126 us (99%)
    pallas_call x1, Pallas kernels, per_device(): pl.pallas_call(kernel, out_shape=[jax.ShapeDtypeStruct((8, 2, B, B), BF),...  125 us

profile of v4, /device:TPU:1, one launch (start us, length us, event | category | flops | bytes accessed | tf_op | source)
XLA Modules:
  0.0 127.1 jit_solution(35366890425340074)
XLA Ops:
  0.6 124.7 %step.1 = (bf16[8,2,256,256]{3,2,1,0:T(8,128)(2,1)S(1)}, bf16[256,256]{1,0:T(8,128)(2,1)S(1)}, bf16[256,128]{1,0:T(8,128)(2,1)S(1)}, bf16[256,128]{1,0:T(8,128)(...) custom-call(bf16[256,4096]{1,0:T(8,128)(2,1)} %bitcast.6, bf16[256,4096]{1,0:T(8,128)(2,1)} %bitcast.7, ...), custom_call_target="tpu_custom_call" | custom-call | tf_op jit(solution)/shard_map/step/pallas_call | solution.py:805
  125.3 1.6 %finish.1 = (bf16[1,256,4096]{2,1,0:T(8,128)(2,1)}, bf16[1,256,256]{2,1,0:T(8,128)(2,1)}, bf16[1,256,128]{2,1,0:T(8,128)(2,1)}, bf16[1,256,128]{2,1,0:T(8,128)(2...) custom-call(bf16[8,2,256,256]{3,2,1,0:T(8,128)(2,1)S(1)} %get-tuple-element.12.og, ...), custom_call_target="tpu_custom_call" | custom-call | tf_op jit(solution)/shard_map/finish/pallas_call | solution.py:825

commit v5 on v4

--- a/solution.py
+++ b/solution.py
@@ -21,8 +21,8 @@
 SCALE = 1.0 / math.sqrt(HD)
 F32 = jnp.float32
 BF = jnp.bfloat16
-RIGHT = (4, 3, 4, 3, 3, 3)
-LEFT = (3, 4, 3, 4, 4, 4)
+RIGHT = (4, 3, 4, 2, 2, 2)
+LEFT = (3, 4, 3, 5, 5, 5)
 
 
 def nt(a, b):
@@ -106,7 +106,7 @@
 
     barrier = pltpu.get_barrier_semaphore()
     greet = [
-        {"z": zr_}, {"z": zl_}, to_y, to_c, {"x": xp}, {"x": xm}, {"x": xa},
+        *[{"z": lax.rem(z + k, NZ)} for k in range(1, NZ)], to_y, to_c, {"x": xp}, {"x": xm}, {"x": xa},
         {"section": psec, "y": py},
     ]
     for dev in greet:
@@ -320,18 +320,21 @@
     drain()
     w_hop(3, (4, 5))
     u_take(1)
-    project(1, 0, 7, HD, HD)
+    project(1, 1, 7, HD, HD)
     u_rest()
+    w_hop(4, late)
     halo(2)
-    w_wait(4, 3)
+    project(2, 1, 7)
     project(1, 7, 8, HD, HD)
+    w_wait(5, 3)
+    project(1, 0, 1, HD, HD)
     project_out(2)
-    project(2, 0, 7)
-    w_wait(4, 4)
-    project(2, 7, 8, 0, HD)
+    project(2, 7, 8)
+    w_wait(5, 4)
+    project(2, 0, 1, 0, HD)
     project_out(3)
-    w_wait(4, 5)
-    project(2, 7, 8, HD, HD)
+    w_wait(5, 5)
+    project(2, 0, 1, HD, HD)
     project_out(4)
     drain()
     halo(3)
@@ -565,6 +568,7 @@
             copy.start()
             sends.append(copy)
 
+    g(1, 0, 2)
     parts(0, own)
     pair_sum(0, own)
     r_send(0, 0, xa, y)
@@ -576,9 +580,9 @@
     arrived(dl.at[1, oth, :], d_s.at[1], d_r.at[1], to_y)
     dlt_make(1)
     g(0, 0, 1)
-    g(1, 0, 2)
     g(1, 0, 1)
     g(0, 1, 2)
+    g(1, 1, 2)
     drain()
 
     query_parts(oth)
@@ -598,7 +602,7 @@
     rds[2] = rds[1] + rdx[0] + rdx[1] + rdx[2]
     send(rds.at[2], rdy, rd_s.at[4], rd_r.at[4], to_y)
     rdb[own, :] = jnp.transpose(jnp.broadcast_to(rds[2, 0:1, :], (HD, B)))
-    g(1, 1, 2)
+    g(1, 1, 1)
     r_send(1, 2, xm, py, 1)
 
     def share(side, first, second, target, k):
@@ -624,10 +628,8 @@
 
     across = {"section": psec, "y": py}
     share(y, (0, 1), (1, 0), rel, 0)
-    g(1, 1, 0)
-    g(0, 1, 0)
     g(0, 2, 2)
-    g(1, 1, 1)
+    g(1, 2, 2)
     arrived(rdy, rd_s.at[4], rd_r.at[4], to_y)
     rdb[oth, :] = jnp.transpose(jnp.broadcast_to(rdy[0:1, :], (HD, B)))
     share(py, (0, 2), (1, 2), og.at[t, y], 1)
@@ -635,24 +637,20 @@
         cut = pl.ds(hf * HD, HD)
         gb[z, :, cut] = jnp.broadcast_to(gain_term(own, cut) + gain_term(oth, cut), (8, HD))
 
-    def gb_send(h):
-        blk = lax.rem(z + NZ - h, NZ)
-        send(gb.at[blk], gb.at[blk], gb_s.at[0, h], gb_r.at[0, h], {"z": zr_})
-        if h < 3:
-            blk = lax.rem(z + h, NZ)
-            send(gb.at[blk], gb.at[blk], gb_s.at[1, h], gb_r.at[1, h], {"z": zl_})
-
-    def gb_wait(h):
-        blk = lax.rem(z + NZ - h, NZ)
-        arrived(gb.at[blk], gb_s.at[0, h - 1], gb_r.at[0, h - 1], {"z": zr_})
-        if h < 4:
-            blk = lax.rem(z + h, NZ)
-            arrived(gb.at[blk], gb_s.at[1, h - 1], gb_r.at[1, h - 1], {"z": zl_})
-
-    gb_send(0)
-    g(1, 2, 0)
-    g(0, 2, 1)
-    drain()
+    for k in range(1, NZ):
+        send(gb.at[z], gb.at[z], gb_s.at[k - 1], gb_r.at[k - 1], {"z": lax.rem(z + k, NZ)})
+
+    def gain_sum():
+        for k in range(1, NZ):
+            arrived(gb.at[lax.rem(z + NZ - k, NZ)], gb_s.at[k - 1], gb_r.at[k - 1], {"z": zr_})
+        gsum = gb[0]
+        for i in range(1, NZ):
+            gsum = gsum + gb[i]
+        gg[y] = gsum
+        send(gg.at[y], gg.at[y], gy_s, gy_r, to_y)
+
+    g(1, 1, 0)
+    g(0, 1, 0)
 
     for q in range(2):
         at = pl.ds(q * HD, HD)
@@ -685,7 +683,7 @@
     def og_wait(blk, par, q, k):
         arrived(og_half(blk, par, q), og_s.at[k, q], og_r.at[k, q], to_c)
 
-    g(0, 2, 0)
+    g(0, 2, 1)
     for q in range(2):
         arrived(og_half(t, py, q), ps_s.at[1, q], ps_r.at[1, q], across)
         og_send(t, py, q, 0, {"x": xp})
@@ -696,22 +694,18 @@
         og_send(t, y, q, 2, {"x": xp})
         og_send(t, y, q, 3, {"x": xm})
         og_send(t, y, q, 7, to_c)
-    g(1, 3, 0)
-    gb_wait(1)
-    gb_send(1)
+    g(1, 2, 0)
+    g(0, 2, 0)
     g(0, 3, 2)
-    g(1, 2, 2)
     for q in range(2):
         og_wait(tr, py, q, 0)
         og_send(tr, py, q, 4, {"x": xp})
         og_send(tr, py, q, 8, to_c)
-    gb_wait(2)
-    gb_send(2)
-    g(1, 2, 1)
-    g(0, 3, 1)
     for q in range(2):
         og_wait(tl, py, q, 1)
         og_send(tl, py, q, 9, to_c)
+    g(1, 2, 1)
+    g(0, 3, 1)
     for q in range(2):
         og_wait(tl, y, q, 3)
         og_send(tl, y, q, 5, {"x": xm})
@@ -719,23 +713,17 @@
     for q in range(2):
         og_wait(tr, y, q, 2)
         og_send(tr, y, q, 10, to_c)
-    gb_wait(3)
-    gb_send(3)
-    drain()
-    finish_grad(2)
-    finish_grad(1)
+    g(1, 3, 0)
     for q in range(2):
         og_wait(ta, py, q, 4)
         og_send(ta, py, q, 12, to_c)
     for q in range(2):
         og_wait(ta, y, q, 5)
         og_send(ta, y, q, 13, to_c)
-    gb_wait(4)
-    gsum = gb[0]
-    for i in range(1, NZ):
-        gsum = gsum + gb[i]
-    gg[y] = gsum
-    send(gg.at[y], gg.at[y], gy_s, gy_r, to_y)
+    gain_sum()
+    finish_grad(2)
+    finish_grad(1)
+    drain()
     finish_grad(0)
     drain()
 
@@ -794,11 +782,11 @@
         vm((2, 3, B, B), BF), vm((2, 3, B, B), BF), vm((2 * B, B), F32), vm((2 * B, B), BF),
         vm((NZ, 8, B), F32),
         dma((7,)), dma, dma, dma,
-        dma((2, 4, 6)), dma((2, 4, 6)), dma((6,)), dma((6,)), dma, dma, dma((5,)), dma((5,)),
+        dma((2, 5, 6)), dma((2, 5, 6)), dma((6,)), dma((6,)), dma, dma, dma((5,)), dma((5,)),
         dma((4, 2)), dma((4, 2)), dma((9, 2)), dma((4, 4)), dma((4, 4)), dma((4, 4)), dma((4, 4)), dma((3,)), dma((3,)),
         dma((5,)), dma((5,)), dma((2, 4, 3)), dma((2, 4, 3)), dma((2, 4)), dma((2, 4)), dma((2, 3, 2)), dma((2, 3, 2)),
         dma((3, 2)), dma((3, 2)),
-        dma((14, 2)), dma((14, 2)), dma((2, 4)), dma((2, 4)), dma, dma,
+        dma((14, 2)), dma((14, 2)), dma((7,)), dma((7,)), dma, dma,
     ]
     hbm = pl.BlockSpec(memory_space=pl.ANY)
     vmem = pl.BlockSpec(memory_space=pltpu.VMEM)

time: 127 us -> 127 us (level)
  no operation moved by 1% of the time
where the time goes in v5:
time: 127 us; the launch traced here: 126 us
  Pallas kernels  126 us (99%)
    pallas_call x1, Pallas kernels, per_device(): pl.pallas_call(kernel, out_shape=[jax.ShapeDtypeStruct((8, 2, B, B), BF),...  124 us

profile of v5, /device:TPU:1, one launch (start us, length us, event | category | flops | bytes accessed | tf_op | source)
XLA Modules:
  0.0 126.4 jit_solution(18085283741998542467)
XLA Ops:
  0.6 124.0 %step.1 = (bf16[8,2,256,256]{3,2,1,0:T(8,128)(2,1)S(1)}, bf16[256,256]{1,0:T(8,128)(2,1)S(1)}, bf16[256,128]{1,0:T(8,128)(2,1)S(1)}, bf16[256,128]{1,0:T(8,128)(...) custom-call(bf16[256,4096]{1,0:T(8,128)(2,1)} %bitcast.6, bf16[256,4096]{1,0:T(8,128)(2,1)} %bitcast.7, ...), custom_call_target="tpu_custom_call" | custom-call | tf_op jit(solution)/shard_map/step/pallas_call | solution.py:793
  124.6 1.6 %finish.1 = (bf16[1,256,4096]{2,1,0:T(8,128)(2,1)}, bf16[1,256,256]{2,1,0:T(8,128)(2,1)}, bf16[1,256,128]{2,1,0:T(8,128)(2,1)}, bf16[1,256,128]{2,1,0:T(8,128)(2...) custom-call(bf16[8,2,256,256]{3,2,1,0:T(8,128)(2,1)S(1)} %get-tuple-element.12.og, ...), custom_call_target="tpu_custom_call" | custom-call | tf_op jit(solution)/shard_map/finish/pallas_call | solution.py:813
